TPU v7x, 32 devices: a whole 2x2x4 slice. The times are simulated.
32 devices in a mesh: parts: 2 (over y), freq: 8 (over z, x), seg: 2 (over core).
Axes of the slice: x: 2, y: 2, z: 4, core: 2. Of those that a mesh axis runs over, the one named last changes fastest.
Arguments:
- samples: float32 [8, 2, 1024, 1024], P(('parts', 'seg'), None, 'freq'), parts along dimension 0, may hold values from -6 to 6
- kernels: bfloat16 [2, 8, 128], replicated, may hold values from -0.375 to 0.375
- offsets: int32 [8, 8], P(('parts', 'seg')), parts along dimension 0, may hold values from -4096 to 4096, as said below
- weight_index: int32 [8], P(('parts', 'seg')), parts along dimension 0, may hold values from 0 to 15
- level_weights: float32 [16], replicated, may hold values from 0.1 to 1
Outputs:
- planes: float32 [16, 1048576], P(('parts', 'seg'), 'freq'), parts along dimension 0
There are 2 independent parts, one for each index of `parts`. A program takes and returns all parts, laid end to end along the dimension named above; an argument that names none is the same for every part. Nothing has to cross between parts.
Inputs may be any that keep to these rules, and one draw needn't show every extreme that they name: `offsets`: each offset lies within 4096 blocks of zero; both ends are taken in every draw. Among the 16 offsets of one index of seg, at most 4 have the same quotient by 1024 (rounded down), and in every draw some quotient has exactly 4.
All inputs are finite; a program needn't handle non-finite values.
Results may differ from a plain program's by a relative error of at most 0.01.
Values may be sent and summed in bfloat16 or wider, within the bound.
No kernel may reach another device: no remote copies, remote signals or barrier semaphores. Data moves between devices by JAX's collectives and lax.ppermute only.
A program may use at most 128 MiB of HBM per device.

v0:
```python
import functools
import math

import jax
import jax.numpy as jnp
import numpy as np
from jax import lax
from jax.experimental import pallas as pl
from jax.experimental.pallas import tpu as pltpu
from jax.sharding import PartitionSpec as P


BLOCK = 128
KERNELS = 8
REACH = 4
ROUTE_CAP = 4
SPLITS = (5,)
FIRST_LIMIT = 60 * 2**20
CHUNK_LIMIT = 34 * 2**20


def extended(cells, sides, width):
    for axis, dim in sides:
        count = lax.axis_size(axis)
        head = lax.slice_in_dim(cells, 0, width, axis=dim)
        tail = lax.slice_in_dim(cells, cells.shape[dim] - width, cells.shape[dim], axis=dim)
        cells = jnp.concatenate(
            [
                lax.ppermute(tail, axis, [(i, (i + 1) % count) for i in range(count)]),
                cells,
                lax.ppermute(head, axis, [((i + 1) % count, i) for i in range(count)]),
            ],
            axis=dim,
        )
    return cells


def passed_along(block, axis, distance):
    devices = range(lax.axis_size(axis))
    route = [((i - distance) % len(devices), i) for i in devices]
    return lax.ppermute(block, axis, route)


def dft_table(size):
    rows = lax.broadcasted_iota(jnp.int32, (size, size), 0)
    cols = lax.broadcasted_iota(jnp.int32, (size, size), 1)
    angle = (rows * cols % size).astype(jnp.float32) * (2.0 * math.pi / size)
    return (jnp.cos(angle), jnp.sin(angle))


def toeplitz(kernels):
    width = kernels.shape[-1]
    tail = jnp.zeros(kernels.shape[:-1] + (width + 1,), kernels.dtype)
    padded = jnp.concatenate([kernels, tail], -1)
    tiled = jnp.tile(padded, (1, 1, width))[..., : 2 * width * width]
    return tiled.reshape(kernels.shape[:-1] + (width, 2 * width))


def take_blocks(joined, start):
    return lax.dynamic_slice_in_dim(joined, start, joined.shape[0] // 2, 0)


def slide(joined, starts):
    return jax.vmap(jax.vmap(take_blocks))(joined, starts)


def spread_body(samples, kernels, offsets, weight_index, level_weights):
    segs, comps, rows_one, cols_two = samples.shape
    ranks = lax.axis_size("freq")
    here = lax.axis_index("freq")
    size_one = rows_one * ranks
    length = size_one * cols_two
    highest = lax.Precision.HIGHEST
    cos_two, sin_two = dft_table(cols_two)
    stacked = samples.reshape(segs * comps * rows_one, cols_two)
    with_cos = jnp.dot(stacked, cos_two, precision=highest).reshape(samples.shape)
    with_sin = jnp.dot(stacked, sin_two, precision=highest).reshape(samples.shape)
    first_real = with_cos[:, 0] + with_sin[:, 1]
    first_imag = with_cos[:, 1] - with_sin[:, 0]
    row_global = here * rows_one + lax.broadcasted_iota(jnp.int32, (rows_one, cols_two), 0)
    col_global = lax.broadcasted_iota(jnp.int32, (rows_one, cols_two), 1)
    twist = (row_global * col_global % length).astype(jnp.float32) * (2.0 * math.pi / length)
    twist_cos = jnp.cos(twist)
    twist_sin = jnp.sin(twist)
    turned = jnp.stack(
        [
            first_real * twist_cos + first_imag * twist_sin,
            first_imag * twist_cos - first_real * twist_sin,
        ],
        1,
    )
    columns = lax.all_to_all(
        turned.astype(jnp.bfloat16), "freq", split_axis=3, concat_axis=3, tiled=True
    ).astype(turned.dtype)
    width_two = cols_two // ranks
    ordered = columns.reshape(segs, comps, rows_one, ranks, width_two)
    cos_one, sin_one = dft_table(size_one)
    cos_one = cos_one.reshape(ranks, rows_one, size_one)
    sin_one = sin_one.reshape(ranks, rows_one, size_one)
    second_cos = jnp.einsum("scirl,rik->sclk", ordered, cos_one, precision=highest)
    second_sin = jnp.einsum("scirl,rik->sclk", ordered, sin_one, precision=highest)
    second = jnp.stack(
        [second_cos[:, 0] + second_sin[:, 1], second_cos[:, 1] - second_sin[:, 0]], 1
    )
    arrived = lax.all_to_all(
        second.astype(jnp.bfloat16), "freq", split_axis=3, concat_axis=3, tiled=True
    ).astype(second.dtype)
    width_one = size_one // ranks
    spectrum = arrived.reshape(segs, comps, width_two, ranks, width_one)
    spectrum = jnp.transpose(spectrum, (0, 1, 4, 3, 2)).reshape(segs, comps, width_one * cols_two)
    spectrum = (spectrum * (1.0 / math.sqrt(length))).astype(jnp.bfloat16)
    half = BLOCK // 2
    edged = extended(spectrum, (("freq", 2),), half)
    bins_here = spectrum.shape[2]
    count = bins_here // BLOCK
    lower = edged[..., :bins_here].reshape(segs, comps, count, BLOCK)
    upper = edged[..., BLOCK:].reshape(segs, comps, count, BLOCK)
    window = jnp.concatenate([lower, upper], -1)
    bands = toeplitz(kernels)
    real_band = bands[0]
    imag_band = bands[1]
    table = jnp.stack(
        [jnp.stack([real_band, imag_band], 0), jnp.stack([-imag_band, real_band], 0)], 0
    )
    filtered = jnp.einsum("scbm,cokim->skboi", window, table, preferred_element_type=jnp.float32)
    power = (filtered[:, :, :, 0] ** 2 + filtered[:, :, :, 1] ** 2).astype(jnp.bfloat16)
    quotient = jnp.floor_divide(offsets, count)
    remainder = offsets - quotient * count
    following = passed_along(power, "freq", -1)
    inner = slide(jnp.concatenate([power, following], 2), remainder)
    plane_count = segs * KERNELS
    flat = inner.reshape(plane_count, count * BLOCK)
    plane_quot = quotient.reshape(plane_count)
    distances = lax.broadcasted_iota(jnp.int32, (2 * REACH + 1, plane_count), 0) - REACH
    member = (plane_quot[None, :] == distances).astype(jnp.int32)
    place = jnp.cumsum(member, 1) - 1
    slot_ids = lax.broadcasted_iota(jnp.int32, (2 * REACH + 1, ROUTE_CAP, plane_count), 1)
    select = ((member[:, None, :] == 1) & (place[:, None, :] == slot_ids)).astype(jnp.bfloat16)
    packed = jnp.einsum("dcp,pl->dcl", select, flat, preferred_element_type=jnp.float32).astype(
        jnp.bfloat16
    )
    received = []
    for step_index in range(2 * REACH + 1):
        received.append(passed_along(packed[step_index], "freq", -(step_index - REACH)))
    gathered = jnp.stack(received, 0)
    placed = jnp.einsum("dcp,dcl->pl", select, gathered, preferred_element_type=jnp.float32)
    shifted = placed.astype(jnp.bfloat16).reshape(segs, KERNELS, count, BLOCK)
    levels = lax.broadcasted_iota(jnp.int32, (segs, level_weights.shape[0]), 1)
    weights = jnp.sum(jnp.where(weight_index[:, None] == levels, level_weights[None, :], 0.0), 1)
    scale = 1.0 / (segs * lax.axis_size("seg"))
    partial_sum = jnp.sum((weights * scale)[:, None, None, None] * shifted.astype(jnp.float32), 0)
    owned = lax.psum_scatter(
        partial_sum.astype(jnp.bfloat16), "seg", scatter_dimension=0, tiled=True
    ).astype(jnp.float32)
    return owned.reshape(owned.shape[0], count * BLOCK)


LINE = 4
PAIR = 2
SUB = 16
GROUP = 32


def phases(products, size):
    angle = (np.asarray(products, np.int64) % size) * (2.0 * math.pi / size)
    return np.cos(angle).astype(np.float32), (-np.sin(angle)).astype(np.float32)


def times(a, b):
    return a[0] * b[0] - a[1] * b[1], a[0] * b[1] + a[1] * b[0]


def vmem():
    return pl.BlockSpec(memory_space=pltpu.VMEM)


def smem():
    return pl.BlockSpec(memory_space=pltpu.SMEM)


def first_kernel(here, x, ar, ai, br, bi, tr, ti, ur, ui, out, er, ei, wr, wi):
    segs, comps, rows, _ = x.shape
    fine = br.shape[0]
    for coarse in range(ar.shape[0]):
        one = (ar[coarse : coarse + 1, :], ai[coarse : coarse + 1, :])
        real, imag = times(one, (br[...], bi[...]))
        er[pl.ds(coarse * fine, fine), :] = real.astype(jnp.bfloat16)
        ei[pl.ds(coarse * fine, fine), :] = imag.astype(jnp.bfloat16)
    step, sub = out.shape[1], out.shape[3]
    series = x[...].astype(jnp.bfloat16).reshape(segs * comps * rows, x.shape[3])
    for table, kept in ((er, wr), (ei, wi)):
        value = jnp.dot(series, table[...], preferred_element_type=jnp.float32)
        for block in range(kept.shape[0]):
            kept[block] = value[:, block * BLOCK : (block + 1) * BLOCK]
    for block in range(wr.shape[0]):
        lanes = slice(block * BLOCK, (block + 1) * BLOCK)
        for turn in range(step):
            twist = times(
                (tr[here[0], turn : turn + 1, lanes], ti[here[0], turn : turn + 1, lanes]),
                (ur[:, lanes], ui[:, lanes]),
            )
            for seg in range(segs):
                low = pl.ds(2 * seg * rows + turn, sub, stride=step)
                high = pl.ds((2 * seg + 1) * rows + turn, sub, stride=step)
                value = (
                    wr[block, low, :] - wi[block, high, :],
                    wi[block, low, :] + wr[block, high, :],
                )
                real, imag = times(value, twist)
                out[seg, turn, 0, :, lanes] = real.astype(jnp.bfloat16)
                out[seg, turn, 1, :, lanes] = imag.astype(jnp.bfloat16)


def first_stage(samples, here, columns, size_one, scale):
    segs, comps, rows, length = samples.shape
    ranks = size_one // rows
    cols = columns.size
    coarse_table = phases(np.arange(length // GROUP)[:, None] * GROUP * columns[None], length)
    fine_table = phases(np.arange(GROUP)[:, None] * columns[None], length)
    outer = np.arange(ranks)[:, None, None] * rows + np.arange(ranks)[None, :, None]
    outer = [
        table * np.float32(scale)
        for table in phases(outer * columns[None, None], size_one * length)
    ]
    sub = rows // ranks
    inner = phases(np.arange(sub)[:, None] * ranks * columns[None], size_one * length)
    return pl.pallas_call(
        first_kernel,
        out_shape=jax.ShapeDtypeStruct((segs, ranks, comps, sub, cols), jnp.bfloat16),
        in_specs=[smem()] + [vmem()] * 9,
        out_specs=vmem(),
        scratch_shapes=[pltpu.VMEM((length, cols), jnp.bfloat16)] * 2
        + [pltpu.VMEM((cols // BLOCK, segs * comps * rows, BLOCK), jnp.float32)] * 2,
        compiler_params=pltpu.CompilerParams(vmem_limit_bytes=FIRST_LIMIT),
        cost_estimate=pl.CostEstimate(
            flops=2 * segs * comps * rows * length * 2 * cols,
            bytes_accessed=4 * samples.size,
            transcendentals=0,
        ),
        name="first_stage",
    )(here, samples, *coarse_table, *fine_table, *outer, *inner)


def gathered(own, tied):
    near = [(i, i ^ PAIR) for i in range(PAIR * LINE)]
    far = [(i, i ^ (2 * PAIR)) for i in range(PAIR * LINE)]
    flip = [(i, i ^ 1) for i in range(PAIR * LINE)]
    middle = [(i, i ^ (3 * PAIR)) for i in range(PAIR, 3 * PAIR)]
    ends = [(i, i ^ PAIR) for i in range(PAIR, 3 * PAIR)]
    half = own.shape[0] // 2

    def send(array, route):
        return lax.ppermute(array, "freq", route)

    by_near = send(own, near)
    crossed = send(own, middle)
    by_flip = send(own, flip)
    by_far = send(own, far)
    low = by_near[:half]
    high = by_flip[half:]
    low, tied = lax.optimization_barrier((low, tied))
    near_low = send(low, flip)
    near_high = send(high, near)
    far_flip = send(by_far, flip)
    relayed = send(by_far, ends)
    by_cross = crossed + relayed
    cross_flip = send(by_cross, flip)
    return [
        (0, own, 0),
        (1, by_flip, 0),
        (PAIR, by_near, 0),
        (PAIR + 1, near_low, 0),
        (PAIR + 1, near_high, half),
        (2 * PAIR, by_far, 0),
        (2 * PAIR + 1, far_flip, 0),
        (3 * PAIR, by_cross, 0),
        (3 * PAIR + 1, cross_flip, 0),
    ], tied


def eight(z):
    root = np.float32(math.sqrt(0.5))

    def add(a, b):
        return a[0] + b[0], a[1] + b[1]

    def sub(a, b):
        return a[0] - b[0], a[1] - b[1]

    def four(a, b, c, d):
        p, q, r, s = add(a, c), sub(a, c), add(b, d), sub(b, d)
        return (
            add(p, r),
            (q[0] + s[1], q[1] - s[0]),
            sub(p, r),
            (q[0] - s[1], q[1] + s[0]),
        )

    even = four(z[0], z[2], z[4], z[6])
    odd = list(four(z[1], z[3], z[5], z[7]))
    x, y = odd[1]
    odd[1] = ((x + y) * root, (y - x) * root)
    x, y = odd[2]
    odd[2] = (y, -x)
    x, y = odd[3]
    odd[3] = ((y - x) * root, -(x + y) * root)
    return [add(even[m], odd[m]) for m in range(4)] + [sub(even[m], odd[m]) for m in range(4)]


def chunk_kernel(plan, *refs):
    pieces, first, last, outs, segs, kinds = plan
    planes = segs * kinds
    refs = list(refs)
    ints, weight = refs.pop(0), refs.pop(0)
    slots = [refs.pop(0) for _ in pieces]
    mats, bands = refs.pop(0), refs.pop(0)
    before = None if first else refs.pop(0)
    total_in = None if first else refs.pop(0)
    after = refs.pop(0) if last else None
    if last:
        mine_out, send_out = refs.pop(0), refs.pop(0)
    else:
        total, edge_out = refs.pop(0), refs.pop(0)
    if first:
        after = refs.pop(0)
    parts, mixed, held, power = (refs.pop(0) for _ in range(4))
    if last:
        total, theirs = refs.pop(0), refs.pop(0)

    def row_start(plane):
        return ints[2 + plane]

    def row_shift(plane):
        return ints[2 + planes + plane]

    def lane_start(plane):
        return ints[2 + 2 * planes + plane]

    for number, (distance, start, length) in enumerate(pieces):
        place = lax.bitwise_xor(ints[0], distance)
        for seg in range(length):
            for turn in range(parts.shape[1]):
                for comp in range(parts.shape[2]):
                    parts[start + seg, turn, comp, place] = slots[number][seg, turn, comp]
    _, step, comps, ranks, sub, cols = parts.shape
    rows = ranks * sub
    count = cols // BLOCK
    size = step * rows
    wrap = held.shape[3] - size
    for seg in range(segs):
        for low in range(0, cols, 2 * BLOCK):
            width = min(2 * BLOCK, cols - low)
            for turn in range(step):
                value = parts[seg, turn, :, :, :, low : low + width]
                mixed[turn, :, :width] = jnp.dot(
                    mats[turn],
                    value.reshape(comps * rows, width),
                    preferred_element_type=jnp.float32,
                )
            for lane in range(0, width, BLOCK):
                block = (low + lane) // BLOCK
                lanes = slice(lane, lane + BLOCK)
                for row in range(0, rows, SUB):
                    z = [
                        (
                            mixed[turn, row : row + SUB, lanes],
                            mixed[turn, rows + row : rows + row + SUB, lanes],
                        )
                        for turn in range(step)
                    ]
                    for turn, value in enumerate(eight(z)):
                        for comp in range(2):
                            one = value[comp].astype(jnp.bfloat16)
                            at = turn * rows + row
                            held[block, seg, comp, at : at + SUB, :] = one
                            if at < wrap:
                                held[block, seg, comp, size + at : size + at + SUB, :] = one
    if not last:
        edge_out[...] = held[count - 1]
    if first:
        for seg in range(segs):
            for comp in range(comps):
                value = held[0, seg, comp, :, :].astype(jnp.float32)
                value = pltpu.roll(value, value.shape[0] - 1, 0).astype(jnp.bfloat16)
                after[seg, comp, :size, :] = value[:size]
                after[seg, comp, size:, :] = value[:wrap]
        total[...] = jnp.zeros_like(total)
    else:
        total[...] = total_in[...]

    def row_block(block, seg, comp, at):
        if block < 0:
            return before[seg, comp, at, :]
        if block == count:
            return after[seg, comp, at, :]
        return held[block, seg, comp, at, :]

    window = power.shape[2]
    for kind in range(kinds):
        real_band, imag_band = bands[0, kind], bands[1, kind]
        table = (
            jnp.concatenate([real_band, imag_band], 1),
            jnp.concatenate([-imag_band, real_band], 1),
        )
        value = None
        for comp in range(2):
            lines = []
            for seg in range(segs):
                at = pl.ds(pl.multiple_of(row_start(seg * kinds + kind), SUB), window)
                for block, _ in outs:
                    lines.append(
                        jnp.concatenate(
                            [row_block(block, seg, comp, at), row_block(block + 1, seg, comp, at)],
                            1,
                        )
                    )
            one = jnp.dot(
                jnp.concatenate(lines, 0), table[comp], preferred_element_type=jnp.float32
            )
            value = one if value is None else value + one
        value = value[:, :BLOCK] ** 2 + value[:, BLOCK:] ** 2
        number = 0
        for seg in range(segs):
            plane = seg * kinds + kind
            lane = lane_start(plane)
            for _, residue in outs:
                power[kind % 2, number] = value[number * window : (number + 1) * window]
                carry = jnp.where(residue < lane, 1, 0)
                place = residue - lane + carry * ranks
                moved = power[kind % 2, number, pl.ds(row_shift(plane) + carry, rows), :]
                total[kind, place] = total[kind, place] + weight[seg] * moved
                number += 1
    if last:
        owned = kinds // 2
        theirs_at = owned * (1 - ints[1])
        mine_at = owned * ints[1]
        for target, base in ((theirs, theirs_at), (mine_out, mine_at)):
            for kind in range(owned):
                for place in range(ranks):
                    at = pl.ds(place * owned + kind, rows, stride=ranks * owned)
                    target[at, :] = total[base + kind, place]
            if target is theirs:
                send_out[...] = theirs[...].astype(jnp.bfloat16)


def chunk(scalars, slots, tables, carried, residues, first, last):
    own = slots[0][1]
    segs, step, comps, sub, cols = own.shape
    ranks = step
    rows = ranks * sub
    size = step * rows
    mats, bands = tables
    kinds = bands.shape[1]
    count = cols // BLOCK
    outs = [] if first else [(-1, residues[0] - 1)]
    outs += [(block, residues[0] + block) for block in range(count - 1)]
    if last:
        outs.append((count - 1, residues[-1]))
    window = rows + SUB
    tall = size + rows
    edge = jax.ShapeDtypeStruct((segs, comps, tall, BLOCK), jnp.bfloat16)
    total = jax.ShapeDtypeStruct((kinds, ranks, rows, BLOCK), jnp.float32)
    flat = (kinds // 2 * ranks * rows, BLOCK)
    if last:
        out_shape = [
            jax.ShapeDtypeStruct(flat, jnp.float32),
            jax.ShapeDtypeStruct(flat, jnp.bfloat16),
        ]
    else:
        out_shape = [total, edge]
    if first:
        out_shape.append(edge)
    pieces = tuple((distance, begin, piece.shape[0]) for distance, piece, begin in slots)
    plan = (pieces, first, last, tuple(outs), segs, kinds)
    arrays = [piece for _, piece, _ in slots]
    inputs = [*scalars, *arrays, mats, bands, *carried]
    specs = [smem()] * 2 + [vmem()] * (len(inputs) - 2)
    scratch = [
        pltpu.VMEM((segs, step, comps, ranks, sub, cols), jnp.bfloat16),
        pltpu.VMEM((step, comps * rows, 2 * BLOCK), jnp.float32),
        pltpu.VMEM((count, segs, comps, tall, BLOCK), jnp.bfloat16),
        pltpu.VMEM((2, segs * len(outs), window, BLOCK), jnp.float32),
    ]
    if last:
        scratch += [pltpu.VMEM(total.shape, total.dtype), pltpu.VMEM(flat, jnp.float32)]
    return pl.pallas_call(
        functools.partial(chunk_kernel, plan),
        out_shape=out_shape,
        in_specs=specs,
        out_specs=[vmem()] * len(out_shape),
        scratch_shapes=scratch,
        compiler_params=pltpu.CompilerParams(vmem_limit_bytes=CHUNK_LIMIT),
        cost_estimate=pl.CostEstimate(
            flops=2 * segs * len(outs) * kinds * window * 4 * BLOCK * 2 * BLOCK
            + 8 * segs * step * rows * rows * cols,
            bytes_accessed=8 * total.size,
            transcendentals=0,
        ),
        name="chunk",
    )(*inputs)


def line_body(samples, kernels, offsets, weight_index, level_weights):
    segs, _, rows, cols_two = samples.shape
    ranks = lax.axis_size("freq")
    size_one = rows * ranks
    length = size_one * cols_two
    kinds = kernels.shape[1]
    blocks_here = length // ranks // BLOCK
    places = jnp.stack([lax.axis_index("freq"), lax.axis_index("seg")]).astype(jnp.int32)
    columns = np.arange(cols_two) - BLOCK // 2
    groups = np.split(np.arange(ranks), SPLITS)
    turned = []
    for group in groups:
        turned.append(
            first_stage(
                samples,
                places,
                columns[group[0] * BLOCK : (group[-1] + 1) * BLOCK],
                size_one,
                1.0 / math.sqrt(length),
            )
        )

    times_of = np.arange(ranks)[:, None, None] + ranks * np.arange(rows)[None, None, :]
    real, imag = phases(times_of * np.arange(rows)[None, :, None], size_one)
    mats = np.concatenate(
        [np.concatenate([real, -imag], 2), np.concatenate([imag, real], 2)], 1
    ).astype(jnp.bfloat16)
    bands = jnp.swapaxes(toeplitz(kernels), -1, -2)

    slots = []
    for own in turned:
        pieces, bands = gathered(own, bands)
        slots.append(pieces)

    bins = jnp.remainder(
        lax.axis_index("freq") * blocks_here + offsets.reshape(segs * kinds), ranks * blocks_here
    )
    row = bins // ranks
    lane = bins - row * ranks
    row_start = row // SUB * SUB
    ints = jnp.concatenate([places, row_start, row - row_start, lane])
    levels = lax.broadcasted_iota(jnp.int32, (segs, level_weights.shape[0]), 1)
    weights = jnp.sum(jnp.where(weight_index[:, None] == levels, level_weights[None, :], 0.0), 1)
    weights = weights * (1.0 / (segs * lax.axis_size("seg")))
    scalars = (ints, weights)

    carried = []
    rolled = None
    for number, group in enumerate(groups):
        first = number == 0
        last = number == len(groups) - 1
        if last:
            carried = carried + [rolled]
        result = chunk(
            scalars, slots[number], (mats, bands), carried, list(group), first, last
        )
        if first:
            rolled = result[2]
        carried = [result[1], result[0]]
    send, own = carried
    other = lax.ppermute(send, "seg", [(i, 1 - i) for i in range(2)])
    out = own + other.astype(jnp.float32)
    owned = kinds // 2
    out = jnp.swapaxes(out.reshape(blocks_here, owned, BLOCK), 0, 1)
    return out.reshape(owned, blocks_here * BLOCK)


def solution(mesh):
    in_specs = (
        P(("parts", "seg"), None, "freq", None),
        P(),
        P(("parts", "seg"), None),
        P(("parts", "seg")),
        P(),
    )
    out_specs = P(("parts", "seg"), "freq")
    line = mesh.shape["freq"] == LINE * PAIR and mesh.shape["seg"] == 2

    def body(samples, *others):
        if not line:
            return spread_body(samples, *others)
        return line_body(samples, *others)

    return jax.shard_map(body, mesh=mesh, in_specs=in_specs, out_specs=out_specs, check_vma=False)
```

profile of v0, /device:TPU:0, one launch (start us, length us, event | category | flops | bytes accessed | tf_op | source)
XLA Modules:
  0.0 168.2 jit_solution(5569533709255951533)
XLA Ops:
  0.0 0.6 pad_add_fusion.here
  0.6 5.1 %first_stage.3.refs_2_ = bf16[2,8,2,16,640]{4,3,2,1,0:T(8,128)(2,1)} custom-call(s32[2]{0:T(128)} %pad_add_fusion.here, f32[2,2,128,1024]{3,2,1,0:T(8,128)} %x.5, f32[32,640]{1,0:T(8,128)} %constant.95.clone.ar, f32[32,640]{1,0:T(8,128)} %constant.96.clone.ai, f32[32,640]{1,0:T(8,128)} %constant.97.clone.br, f32[32,640]{1,0:T(8,128)} %constant.98.clone.bi, ...), custom_call_target="tpu_custom_call" | custom-call | flops 1342177280 | bytes 2097152 | tf_op jit(solution)/shard_map/first_stage/pallas_call | solution.py:227
  5.6 4.1 %collective-permute-start.13 = (bf16[2,8,2,16,640]{4,3,2,1,0:T(8,128)(2,1)}, bf16[2,8,2,16,640]{4,3,2,1,0:T(8,128)(2,1)}, u32[]{:S(2)}, u32[]{:S(2)}) collective-permute-start(bf16[2,8,2,16,640]{4,3,2,1,0:T(8,128)(2,1)} %first_stage.3.refs_2_), channel_id=1, source_target_pairs={{0,8},{2,10},{4,12},{6,14},{8,0},{10,2},{12,4},{14,6},{1,9},{3,11}... | collective-permute-start | bytes 1966088 | tf_op jit(solution)/shard_map/ppermute | solution.py:253
  9.7 0.7 collective-permute-start.15
  10.4 29.2 %collective-permute-done.13.refs_7_ = bf16[2,8,2,16,640]{4,3,2,1,0:T(8,128)(2,1)} collective-permute-done((bf16[2,8,2,16,640]{4,3,2,1,0:T(8,128)(2,1)}, bf16[2,8,2,16,640]{4,3,2,1,0:T(8,128)(2,1)}, u32[]{:S(2)}, u32[]{:S(2)}) %collective-permute-start.13) | collective-permute-done | bytes 655392 | tf_op jit(solution)/shard_map/ppermute | solution.py:253
  39.7 1.3 collective-permute-start.16
  40.9 3.5 %collective-permute-start.2 = (bf16[2,8,2,16,640]{4,3,2,1,0:T(8,128)(2,1)}, bf16[2,8,2,16,640]{4,3,2,1,0:T(8,128)(2,1)S(1)}, u32[]{:S(2)}, u32[]{:S(2)}) collective-permute-start(bf16[2,8,2,16,640]{4,3,2,1,0:T(8,128)(2,1)} %first_stage.3.refs_2_), channel_id=1, source_target_pairs={{0,4},{2,6},{4,0},{6,2},{8,12},{10,14},{12,8},{14,10},{1,5},{3,7},... | collective-permute-start | bytes 1966088 | tf_op jit(solution)/shard_map/ppermute | solution.py:253
  44.4 1.8 %collective-permute-start.10 = (bf16[2,8,2,16,640]{4,3,2,1,0:T(8,128)(2,1)}, bf16[2,8,2,16,640]{4,3,2,1,0:T(8,128)(2,1)S(1)}, u32[]{:S(2)}, u32[]{:S(2)}) collective-permute-start(bf16[2,8,2,16,640]{4,3,2,1,0:T(8,128)(2,1)} %first_stage.3.refs_2_), channel_id=1, source_target_pairs={{0,2},{2,0},{4,6},{6,4},{8,10},{10,8},{12,14},{14,12},{1,3},{3,1},... | collective-permute-start | bytes 1966088 | tf_op jit(solution)/shard_map/ppermute | solution.py:253
  46.2 4.1 %first_stage.2.refs_2_ = bf16[2,8,2,16,384]{4,3,2,1,0:T(8,128)(2,1)} custom-call(s32[2]{0:T(128)} %pad_add_fusion.here, f32[2,2,128,1024]{3,2,1,0:T(8,128)} %x.5, f32[32,384]{1,0:T(8,128)} %constant.103.clone.ar, f32[32,384]{1,0:T(8,128)} %constant.104.clone.ai, f32[32,384]{1,0:T(8,128)} %constant.105.clone.br, f32[32,384]{1,0:T(8,128)} %constant.106.clone.bi, ...), custom_call_target="tpu_custom_call" | custom-call | flops 805306368 | bytes 2097152 | tf_op jit(solution)/shard_map/first_stage/pallas_call | solution.py:227
  50.4 0.0 collective-permute-start.1
  50.4 5.0 %collective-permute-start.5 = (bf16[2,8,2,16,384]{4,3,2,1,0:T(8,128)(2,1)}, bf16[2,8,2,16,384]{4,3,2,1,0:T(8,128)(2,1)S(1)}, u32[]{:S(2)}, u32[]{:S(2)}) collective-permute-start(bf16[2,8,2,16,384]{4,3,2,1,0:T(8,128)(2,1)} %first_stage.2.refs_2_), channel_id=1, source_target_pairs={{0,8},{2,10},{4,12},{6,14},{8,0},{10,2},{12,4},{14,6},{1,9},{3,11}... | collective-permute-start | bytes 1179656 | tf_op jit(solution)/shard_map/ppermute | solution.py:253
  55.4 12.5 %collective-permute-done.16 = bf16[2,8,2,16,640]{4,3,2,1,0:T(8,128)(2,1)} collective-permute-done((bf16[2,8,2,16,640]{4,3,2,1,0:T(8,128)(2,1)}, bf16[2,8,2,16,640]{4,3,2,1,0:T(8,128)(2,1)}, u32[]{:S(2)}, u32[]{:S(2)}) %collective-permute-start.16) | collective-permute-done | bytes 655392 | tf_op jit(solution)/shard_map/ppermute | solution.py:253
  67.9 1.4 collective-permute-start.7
  69.3 0.1 add.30
  69.4 1.2 add.33.refs_9_
  70.7 17.0 %collective-permute-done.1.refs_4_ = bf16[2,8,2,16,384]{4,3,2,1,0:T(8,128)(2,1)S(1)} collective-permute-done((bf16[2,8,2,16,384]{4,3,2,1,0:T(8,128)(2,1)}, bf16[2,8,2,16,384]{4,3,2,1,0:T(8,128)(2,1)S(1)}, u32[]{:S(2)}, u32[]{:S(2)}) %collective-permute-start.1) | collective-permute-done | bytes 393248 | tf_op jit(solution)/shard_map/ppermute | solution.py:253
  87.7 1.3 collective-permute-start
  89.0 1.3 collective-permute-start.8
  90.3 0.8 collective-permute-start.14
  91.1 1.3 collective-permute-start.17
  92.4 1.3 tile.4
  93.7 3.8 %tile.10 = bf16[2,8,32896]{2,1,0:T(8,128)(2,1)} reshape(bf16[2,8,128,257]{3,2,1,0:T(8,128)(2,1)} %tile.4) | data formatting | bytes 2105344 | tf_op jit(solution)/shard_map/tile | solution.py:55
  97.6 1.2 slice-done
  98.8 1.2 copy.30
  100.0 1.8 %copy.26 = bf16[2,8,128,256]{2,3,1,0:T(8,128)(2,1)S(1)} copy(bf16[2,8,128,256]{3,2,1,0:T(8,128)(2,1)} %copy.30) | data formatting | bytes 2097152 | tf_op jit(solution)/shard_map/reshape | solution.py:56
  101.9 0.8 collective-permute-start.11
  102.7 0.8 slice.24
  103.4 3.3 %collective-permute-start.12 = (bf16[1,8,2,16,640]{4,3,2,1,0:T(8,128)(2,1)}, bf16[1,8,2,16,640]{4,3,2,1,0:T(8,128)(2,1)}, u32[]{:S(2)}, u32[]{:S(2)}) collective-permute-start(bf16[1,8,2,16,640]{4,3,2,1,0:T(8,128)(2,1)} %slice.24), channel_id=1, source_target_pairs={{0,4},{2,6},{4,0},{6,2},{8,12},{10,14},{12,8},{14,10},{1,5},{3,7},... | collective-permute-start | bytes 983048 | tf_op jit(solution)/shard_map/ppermute | solution.py:253
  106.8 0.2 fusion
  106.9 1.2 add.32.refs_9_
  108.2 1.4 collective-permute-start.6
  109.5 25.5 %collective-permute-done.11.refs_5_ = bf16[1,8,2,16,640]{4,3,2,1,0:T(8,128)(2,1)S(1)} collective-permute-done((bf16[1,8,2,16,640]{4,3,2,1,0:T(8,128)(2,1)S(1)}, bf16[1,8,2,16,640]{4,3,2,1,0:T(8,128)(2,1)S(1)}, u32[]{:S(2)}, u32[]{:S(2)}) %collective-permute-start.11) | collective-permute-done | bytes 327712 | tf_op jit(solution)/shard_map/ppermute | solution.py:253
  135.0 0.7 copy-done.6
  135.7 1.3 collective-permute-start.9
  137.0 0.1 concatenate.7.refs_0_
  137.1 1.0 slice.20
  138.1 1.0 slice.23
  139.1 0.1 collective-permute-start.4
  139.2 0.8 collective-permute-start.3
  140.0 1.1 copy-done.2
  141.1 1.0 copy-done.7
  142.1 1.2 copy-done.8
  143.3 8.6 %chunk.2 = (f32[8,8,128,128]{3,2,1,0:T(8,128)S(1)}, bf16[2,2,1152,128]{3,2,1,0:T(8,128)(2,1)S(1)}, bf16[2,2,1152,128]{3,2,1,0:T(8,128)(2,1)S(1)}) custom-call(s32[50]{0:T(128)S(1)} %concatenate.7.refs_0_, f32[2]{0:T(128)S(1)} %broadcast_multiply_fusion.refs_1_, bf16[2,8,2,16,640]{4,3,2,1,0:T(8,128)(2,1)S(1)} %copy-done.2, ...), custom_call_target="tpu_custom_call" | custom-call | flops 3758096384 | bytes 8388608 | tf_op jit(solution)/shard_map/chunk/pallas_call | solution.py:486
  151.9 0.7 collective-permute-done.3.refs_5_
  152.7 11.2 %chunk.3 = (f32[4096,128]{1,0:T(8,128)S(1)}, bf16[4096,128]{1,0:T(8,128)(2,1)S(1)}) custom-call(s32[50]{0:T(128)S(1)} %concatenate.7.refs_0_, f32[2]{0:T(128)S(1)} %broadcast_multiply_fusion.refs_1_, bf16[2,8,2,16,384]{4,3,2,1,0:T(8,128)(2,1)S(1)} %copy-done.3, bf16[2,8,2,16,384]{4,3,2,1,0:T(8,128)(2,1)} %collective-permute-done.refs_3_, ...), custom_call_target="tpu_custom_call" | custom-call | flops 3221225472 | bytes 8388608 | tf_op jit(solution)/shard_map/chunk/pallas_call | solution.py:486
  163.9 0.1 collective-permute-start.18
  163.9 2.6 %collective-permute-done.18 = bf16[4096,128]{1,0:T(8,128)(2,1)S(1)} collective-permute-done((bf16[4096,128]{1,0:T(8,128)(2,1)S(1)}, bf16[4096,128]{1,0:T(8,128)(2,1)S(1)}, u32[]{:S(2)}, u32[]{:S(2)}) %collective-permute-start.18) | collective-permute-done | bytes 1048608 | tf_op jit(solution)/shard_map/ppermute | solution.py:563
  166.6 1.6 convert_add_fusion
  (44 shorter events, 0.1 us)
Async XLA Ops:
  5.6 63.7 %copy-start.11 = (s32[2,8]{1,0:T(2,128)S(1)}, s32[2,8]{1,0:T(2,128)}, u32[]{:S(2)}) copy-start(s32[2,8]{1,0:T(2,128)} %param.24) | copy-start | bytes 196
  5.6 86.8 %copy-start.10 = (bf16[2,8,128]{2,1,0:T(8,128)(2,1)S(1)}, bf16[2,8,128]{2,1,0:T(8,128)(2,1)}, u32[]{:S(2)}) copy-start(bf16[2,8,128]{2,1,0:T(8,128)(2,1)} %param.23) | copy-start | bytes 12292
  5.6 34.0 %collective-permute-start.13 = (bf16[2,8,2,16,640]{4,3,2,1,0:T(8,128)(2,1)}, bf16[2,8,2,16,640]{4,3,2,1,0:T(8,128)(2,1)}, u32[]{:S(2)}, u32[]{:S(2)}) collective-permute-start(bf16[2,8,2,16,640]{4,3,2,1,0:T(8,128)(2,1)} %first_stage.3.refs_2_), channel_id=1, source_target_pairs={{0,8},{2,10},{4,12},{6,14},{8,0},{10,2},{12,4},{14,6},{1,9},{3,11}... | collective-permute-start | bytes 1966088 | tf_op jit(solution)/shard_map/ppermute | solution.py:253
  9.7 40.7 %collective-permute-start.15 = (bf16[2,8,2,16,640]{4,3,2,1,0:T(8,128)(2,1)}, bf16[2,8,2,16,640]{4,3,2,1,0:T(8,128)(2,1)S(1)}, u32[]{:S(2)}, u32[]{:S(2)}) collective-permute-start(bf16[2,8,2,16,640]{4,3,2,1,0:T(8,128)(2,1)} %first_stage.3.refs_2_), channel_id=1, source_target_pairs={{4,8},{6,10},{8,4},{10,6},{5,9},{7,11},{9,5},{11,7},{20,24},{22,26... | collective-permute-start | bytes 1966088 | tf_op jit(solution)/shard_map/ppermute | solution.py:253
  39.7 28.2 %collective-permute-start.16 = (bf16[2,8,2,16,640]{4,3,2,1,0:T(8,128)(2,1)}, bf16[2,8,2,16,640]{4,3,2,1,0:T(8,128)(2,1)}, u32[]{:S(2)}, u32[]{:S(2)}) collective-permute-start(bf16[2,8,2,16,640]{4,3,2,1,0:T(8,128)(2,1)} %collective-permute-done.13.refs_7_), channel_id=1, source_target_pairs={{4,0},{6,2},{8,12},{10,14},{5,1},{7,3},{9,13},{11,15},{20,16},{22,... | collective-permute-start | bytes 1966088 | tf_op jit(solution)/shard_map/ppermute | solution.py:253
  40.9 50.1 %collective-permute-start.2 = (bf16[2,8,2,16,640]{4,3,2,1,0:T(8,128)(2,1)}, bf16[2,8,2,16,640]{4,3,2,1,0:T(8,128)(2,1)S(1)}, u32[]{:S(2)}, u32[]{:S(2)}) collective-permute-start(bf16[2,8,2,16,640]{4,3,2,1,0:T(8,128)(2,1)} %first_stage.3.refs_2_), channel_id=1, source_target_pairs={{0,4},{2,6},{4,0},{6,2},{8,12},{10,14},{12,8},{14,10},{1,5},{3,7},... | collective-permute-start | bytes 1966088 | tf_op jit(solution)/shard_map/ppermute | solution.py:253
  44.4 57.4 %collective-permute-start.10 = (bf16[2,8,2,16,640]{4,3,2,1,0:T(8,128)(2,1)}, bf16[2,8,2,16,640]{4,3,2,1,0:T(8,128)(2,1)S(1)}, u32[]{:S(2)}, u32[]{:S(2)}) collective-permute-start(bf16[2,8,2,16,640]{4,3,2,1,0:T(8,128)(2,1)} %first_stage.3.refs_2_), channel_id=1, source_target_pairs={{0,2},{2,0},{4,6},{6,4},{8,10},{10,8},{12,14},{14,12},{1,3},{3,1},... | collective-permute-start | bytes 1966088 | tf_op jit(solution)/shard_map/ppermute | solution.py:253
  50.4 37.3 %collective-permute-start.1 = (bf16[2,8,2,16,384]{4,3,2,1,0:T(8,128)(2,1)}, bf16[2,8,2,16,384]{4,3,2,1,0:T(8,128)(2,1)S(1)}, u32[]{:S(2)}, u32[]{:S(2)}) collective-permute-start(bf16[2,8,2,16,384]{4,3,2,1,0:T(8,128)(2,1)} %first_stage.2.refs_2_), channel_id=1, source_target_pairs={{0,4},{2,6},{4,0},{6,2},{8,12},{10,14},{12,8},{14,10},{1,5},{3,7},... | collective-permute-start | bytes 1179656 | tf_op jit(solution)/shard_map/ppermute | solution.py:253
  50.4 38.6 %collective-permute-start.5 = (bf16[2,8,2,16,384]{4,3,2,1,0:T(8,128)(2,1)}, bf16[2,8,2,16,384]{4,3,2,1,0:T(8,128)(2,1)S(1)}, u32[]{:S(2)}, u32[]{:S(2)}) collective-permute-start(bf16[2,8,2,16,384]{4,3,2,1,0:T(8,128)(2,1)} %first_stage.2.refs_2_), channel_id=1, source_target_pairs={{0,8},{2,10},{4,12},{6,14},{8,0},{10,2},{12,4},{14,6},{1,9},{3,11}... | collective-permute-start | bytes 1179656 | tf_op jit(solution)/shard_map/ppermute | solution.py:253
  67.9 22.4 %collective-permute-start.7 = (bf16[2,8,2,16,384]{4,3,2,1,0:T(8,128)(2,1)}, bf16[2,8,2,16,384]{4,3,2,1,0:T(8,128)(2,1)}, u32[]{:S(2)}, u32[]{:S(2)}) collective-permute-start(bf16[2,8,2,16,384]{4,3,2,1,0:T(8,128)(2,1)} %first_stage.2.refs_2_), channel_id=1, source_target_pairs={{4,8},{6,10},{8,4},{10,6},{5,9},{7,11},{9,5},{11,7},{20,24},{22,26... | collective-permute-start | bytes 1179656 | tf_op jit(solution)/shard_map/ppermute | solution.py:253
  87.7 9.9 %copy-start = (bf16[2,8,2,16,384]{4,3,2,1,0:T(8,128)(2,1)}, bf16[2,8,2,16,384]{4,3,2,1,0:T(8,128)(2,1)S(1)}, u32[]{:S(2)}) copy-start(bf16[2,8,2,16,384]{4,3,2,1,0:T(8,128)(2,1)S(1)} %collective-permute-done.1.refs_4_) | copy-start | bytes 1179652
  87.7 20.5 %collective-permute-start = (bf16[2,8,2,16,384]{4,3,2,1,0:T(8,128)(2,1)}, bf16[2,8,2,16,384]{4,3,2,1,0:T(8,128)(2,1)}, u32[]{:S(2)}, u32[]{:S(2)}) collective-permute-start(bf16[2,8,2,16,384]{4,3,2,1,0:T(8,128)(2,1)} %first_stage.2.refs_2_), channel_id=1, source_target_pairs={{0,2},{2,0},{4,6},{6,4},{8,10},{10,8},{12,14},{14,12},{1,3},{3,1},... | collective-permute-start | bytes 1179656 | tf_op jit(solution)/shard_map/ppermute | solution.py:253
  89.0 17.8 %copy-start.4 = (bf16[2,8,2,16,384]{4,3,2,1,0:T(8,128)(2,1)}, bf16[2,8,2,16,384]{4,3,2,1,0:T(8,128)(2,1)S(1)}, u32[]{:S(2)}) copy-start(bf16[2,8,2,16,384]{4,3,2,1,0:T(8,128)(2,1)S(1)} %collective-permute-done.5.refs_7_) | copy-start | bytes 1179652
  89.0 14.4 %collective-permute-start.8 = (bf16[2,8,2,16,384]{4,3,2,1,0:T(8,128)(2,1)S(1)}, bf16[2,8,2,16,384]{4,3,2,1,0:T(8,128)(2,1)}, u32[]{:S(2)}, u32[]{:S(2)}) collective-permute-start(bf16[2,8,2,16,384]{4,3,2,1,0:T(8,128)(2,1)S(1)} %collective-permute-done.5.refs_7_), channel_id=1, source_target_pairs={{4,0},{6,2},{8,12},{10,14},{5,1},{7,3},{9,13},{11,15},{20,16},{22,... | collective-permute-start | bytes 1179656 | tf_op jit(solution)/shard_map/ppermute | solution.py:253
  90.3 48.9 %collective-permute-start.14 = (bf16[2,8,2,16,640]{4,3,2,1,0:T(8,128)(2,1)}, bf16[2,8,2,16,640]{4,3,2,1,0:T(8,128)(2,1)}, u32[]{:S(2)}, u32[]{:S(2)}) collective-permute-start(bf16[2,8,2,16,640]{4,3,2,1,0:T(8,128)(2,1)} %collective-permute-done.13.refs_7_), channel_id=1, source_target_pairs={{0,2},{2,0},{4,6},{6,4},{8,10},{10,8},{12,14},{14,12},{1,3},{3,1},... | collective-permute-start | bytes 1966088 | tf_op jit(solution)/shard_map/ppermute | solution.py:253
  91.1 48.9 %collective-permute-start.17 = (bf16[2,8,2,16,640]{4,3,2,1,0:T(8,128)(2,1)S(1)}, bf16[2,8,2,16,640]{4,3,2,1,0:T(8,128)(2,1)}, u32[]{:S(2)}, u32[]{:S(2)}) collective-permute-start(bf16[2,8,2,16,640]{4,3,2,1,0:T(8,128)(2,1)S(1)} %add.33.refs_9_), channel_id=1, source_target_pairs={{0,2},{2,0},{4,6},{6,4},{8,10},{10,8},{12,14},{14,12},{1,3},{3,1},... | collective-permute-start | bytes 1966088 | tf_op jit(solution)/shard_map/ppermute | solution.py:253
  97.6 1.2 slice-start
  100.0 6.8 %copy-start.12 = (f32[16]{0:T(128)S(1)}, f32[16]{0:T(128)}, u32[]{:S(2)}) copy-start(f32[16]{0:T(128)} %param.26) | copy-start | bytes 196
  100.0 6.8 %copy-start.13 = (s32[2]{0:T(128)S(1)}, s32[2]{0:T(128)}, u32[]{:S(2)}) copy-start(s32[2]{0:T(128)} %param.25) | copy-start | bytes 28
  101.9 33.1 %collective-permute-start.11 = (bf16[1,8,2,16,640]{4,3,2,1,0:T(8,128)(2,1)S(1)}, bf16[1,8,2,16,640]{4,3,2,1,0:T(8,128)(2,1)S(1)}, u32[]{:S(2)}, u32[]{:S(2)}) collective-permute-start(bf16[1,8,2,16,640]{4,3,2,1,0:T(8,128)(2,1)S(1)} %slice.21), channel_id=1, source_target_pairs={{0,2},{2,0},{4,6},{6,4},{8,10},{10,8},{12,14},{14,12},{1,3},{3,1},... | collective-permute-start | bytes 983048 | tf_op jit(solution)/shard_map/ppermute | solution.py:253
  103.4 35.7 %collective-permute-start.12 = (bf16[1,8,2,16,640]{4,3,2,1,0:T(8,128)(2,1)}, bf16[1,8,2,16,640]{4,3,2,1,0:T(8,128)(2,1)}, u32[]{:S(2)}, u32[]{:S(2)}) collective-permute-start(bf16[1,8,2,16,640]{4,3,2,1,0:T(8,128)(2,1)} %slice.24), channel_id=1, source_target_pairs={{0,4},{2,6},{4,0},{6,2},{8,12},{10,14},{12,8},{14,10},{1,5},{3,7},... | collective-permute-start | bytes 983048 | tf_op jit(solution)/shard_map/ppermute | solution.py:253
  108.2 43.7 %collective-permute-start.6 = (bf16[2,8,2,16,384]{4,3,2,1,0:T(8,128)(2,1)}, bf16[2,8,2,16,384]{4,3,2,1,0:T(8,128)(2,1)}, u32[]{:S(2)}, u32[]{:S(2)}) collective-permute-start(bf16[2,8,2,16,384]{4,3,2,1,0:T(8,128)(2,1)} %copy-done.4), channel_id=1, source_target_pairs={{0,2},{2,0},{4,6},{6,4},{8,10},{10,8},{12,14},{14,12},{1,3},{3,1},... | collective-permute-start | bytes 1179656 | tf_op jit(solution)/shard_map/ppermute | solution.py:253
  135.0 0.7 copy-start.6
  135.7 16.9 %collective-permute-start.9 = (bf16[2,8,2,16,384]{4,3,2,1,0:T(8,128)(2,1)S(1)}, bf16[2,8,2,16,384]{4,3,2,1,0:T(8,128)(2,1)}, u32[]{:S(2)}, u32[]{:S(2)}) collective-permute-start(bf16[2,8,2,16,384]{4,3,2,1,0:T(8,128)(2,1)S(1)} %add.32.refs_9_), channel_id=1, source_target_pairs={{0,2},{2,0},{4,6},{6,4},{8,10},{10,8},{12,14},{14,12},{1,3},{3,1},... | collective-permute-start | bytes 1179656 | tf_op jit(solution)/shard_map/ppermute | solution.py:253
  137.1 15.5 %copy-start.5 = (bf16[2,8,2,16,384]{4,3,2,1,0:T(8,128)(2,1)S(1)}, bf16[2,8,2,16,384]{4,3,2,1,0:T(8,128)(2,1)}, u32[]{:S(2)}) copy-start(bf16[2,8,2,16,384]{4,3,2,1,0:T(8,128)(2,1)} %copy-done.4) | copy-start | bytes 1179652
  138.1 14.5 %copy-start.3 = (bf16[2,8,2,16,384]{4,3,2,1,0:T(8,128)(2,1)S(1)}, bf16[2,8,2,16,384]{4,3,2,1,0:T(8,128)(2,1)}, u32[]{:S(2)}) copy-start(bf16[2,8,2,16,384]{4,3,2,1,0:T(8,128)(2,1)} %first_stage.2.refs_2_) | copy-start | bytes 1179652
  139.1 13.5 %copy-start.1 = (bf16[2,8,2,16,384]{4,3,2,1,0:T(8,128)(2,1)S(1)}, bf16[2,8,2,16,384]{4,3,2,1,0:T(8,128)(2,1)}, u32[]{:S(2)}) copy-start(bf16[2,8,2,16,384]{4,3,2,1,0:T(8,128)(2,1)} %copy-done) | copy-start | bytes 1179652
  139.1 12.7 %collective-permute-start.4 = (bf16[1,8,2,16,384]{4,3,2,1,0:T(8,128)(2,1)S(1)}, bf16[1,8,2,16,384]{4,3,2,1,0:T(8,128)(2,1)S(1)}, u32[]{:S(2)}, u32[]{:S(2)}) collective-permute-start(bf16[1,8,2,16,384]{4,3,2,1,0:T(8,128)(2,1)S(1)} %slice.23), channel_id=1, source_target_pairs={{0,4},{2,6},{4,0},{6,2},{8,12},{10,14},{12,8},{14,10},{1,5},{3,7},... | collective-permute-start | bytes 589832 | tf_op jit(solution)/shard_map/ppermute | solution.py:253
  139.2 13.4 %collective-permute-start.3 = (bf16[1,8,2,16,384]{4,3,2,1,0:T(8,128)(2,1)S(1)}, bf16[1,8,2,16,384]{4,3,2,1,0:T(8,128)(2,1)S(1)}, u32[]{:S(2)}, u32[]{:S(2)}) collective-permute-start(bf16[1,8,2,16,384]{4,3,2,1,0:T(8,128)(2,1)S(1)} %slice.20), channel_id=1, source_target_pairs={{0,2},{2,0},{4,6},{6,4},{8,10},{10,8},{12,14},{14,12},{1,3},{3,1},... | collective-permute-start | bytes 589832 | tf_op jit(solution)/shard_map/ppermute | solution.py:253
  140.0 1.1 copy-start.2
  141.1 1.0 copy-start.7
  142.1 1.2 copy-start.8
  143.3 9.3 %copy-start.9 = (bf16[8,256,256]{2,1,0:T(8,128)(2,1)S(1)}, bf16[8,256,256]{2,1,0:T(8,128)(2,1)}, u32[]{:S(2)}) copy-start(bf16[8,256,256]{2,1,0:T(8,128)(2,1)} %constant.111.clone.refs_11_) | copy-start | bytes 3145732
  163.9 2.7 %collective-permute-start.18 = (bf16[4096,128]{1,0:T(8,128)(2,1)S(1)}, bf16[4096,128]{1,0:T(8,128)(2,1)S(1)}, u32[]{:S(2)}, u32[]{:S(2)}) collective-permute-start(bf16[4096,128]{1,0:T(8,128)(2,1)S(1)} %get-tuple-element.22), channel_id=1, source_target_pairs={{0,1},{1,0},{2,3},{3,2},{4,5},{5,4},{6,7},{7,6},{8,9},{9,8},{10,11... | collective-permute-start | bytes 3145736 | tf_op jit(solution)/shard_map/ppermute | solution.py:563
where the time goes:
time: 170 us; the launch traced here: 168 us
  waiting for transfers between devices  87.6 us (52%)
  starting transfers between devices  30.2 us (18%)
  Pallas kernels  28.9 us (17%)
  local copies, waits for them, and re-layouts  16.4 us (10%)
  other arithmetic  4.85 us (3%)
    ppermute x18, waiting for transfers between devices, send(): return lax.ppermute(array, 'freq', route)  85 us
    ppermute x18, starting transfers between devices, send(): return lax.ppermute(array, 'freq', route)  30.1 us
    pallas_call x2, Pallas kernels, chunk(): pl.pallas_call(functools.partial(chunk_kernel, plan), out_shape=out_shape...  19.7 us
    pallas_call x2, Pallas kernels, first_stage(): pl.pallas_call(first_kernel, out_shape=jax.ShapeDtypeStruct((segs, ranks,...  9.18 us
    unnamed x29, local copies, waits for them, and re-layouts  5.25 us
    another operation x2, local copies, waits for them, and re-layouts, toeplitz(): tiled = jnp.tile(padded, (1, 1, width))[..., :2 * width * width]  5.13 us
  transfers between devices with their start and end apart: 19, of which 6 were waited for; matrix products, arithmetic and copies ran while one was open for 8% of the time, Pallas kernels for 8%

commit v1 on v0

--- a/solution.py
+++ b/solution.py
@@ -14,7 +14,7 @@
 KERNELS = 8
 REACH = 4
 ROUTE_CAP = 4
-SPLITS = (5,)
+SPLITS = (4,)
 FIRST_LIMIT = 60 * 2**20
 CHUNK_LIMIT = 34 * 2**20
 
@@ -178,59 +178,83 @@
     return pl.BlockSpec(memory_space=pltpu.SMEM)
 
 
-def first_kernel(here, x, ar, ai, br, bi, tr, ti, ur, ui, out, er, ei, wr, wi):
-    segs, comps, rows, _ = x.shape
-    fine = br.shape[0]
-    for coarse in range(ar.shape[0]):
-        one = (ar[coarse : coarse + 1, :], ai[coarse : coarse + 1, :])
-        real, imag = times(one, (br[...], bi[...]))
+def first_kernel(begin, heights, x_hbm, tables_hbm, out, x, tables, er, ei, wr, wi, sems):
+    segs, comps, rows, length = x.shape
+    step, sub, cols = out.shape[1], out.shape[3], out.shape[4]
+    copies = [
+        pltpu.make_async_copy(tables_hbm.at[:, pl.ds(begin, cols)], tables, sems.at[segs])
+    ]
+    for seg in range(segs):
+        copies.append(pltpu.make_async_copy(x_hbm.at[seg], x.at[seg], sems.at[seg]))
+    for copy in copies:
+        copy.start()
+    here = lax.axis_index("freq")
+    at = np.concatenate([[0], np.cumsum(heights)])
+
+    def table(number, row=0, height=None):
+        height = heights[number] if height is None else height
+        return tables[pl.ds(int(at[number]) + row, height), :]
+
+    fine = heights[2]
+    copies[0].wait()
+    inner = (table(2), table(3))
+    for coarse in range(heights[0]):
+        real, imag = times((table(0, coarse, 1), table(1, coarse, 1)), inner)
         er[pl.ds(coarse * fine, fine), :] = real.astype(jnp.bfloat16)
         ei[pl.ds(coarse * fine, fine), :] = imag.astype(jnp.bfloat16)
-    step, sub = out.shape[1], out.shape[3]
-    series = x[...].astype(jnp.bfloat16).reshape(segs * comps * rows, x.shape[3])
-    for table, kept in ((er, wr), (ei, wi)):
-        value = jnp.dot(series, table[...], preferred_element_type=jnp.float32)
-        for block in range(kept.shape[0]):
-            kept[block] = value[:, block * BLOCK : (block + 1) * BLOCK]
-    for block in range(wr.shape[0]):
-        lanes = slice(block * BLOCK, (block + 1) * BLOCK)
-        for turn in range(step):
-            twist = times(
-                (tr[here[0], turn : turn + 1, lanes], ti[here[0], turn : turn + 1, lanes]),
-                (ur[:, lanes], ui[:, lanes]),
-            )
-            for seg in range(segs):
-                low = pl.ds(2 * seg * rows + turn, sub, stride=step)
-                high = pl.ds((2 * seg + 1) * rows + turn, sub, stride=step)
+    for seg in range(segs):
+        copies[1 + seg].wait()
+        series = x[seg].astype(jnp.bfloat16).reshape(comps * rows, length)
+        for phase, kept in ((er, wr), (ei, wi)):
+            value = jnp.dot(series, phase[...], preferred_element_type=jnp.float32)
+            for block in range(kept.shape[1]):
+                kept[seg, block] = value[:, block * BLOCK : (block + 1) * BLOCK]
+        for block in range(wr.shape[1]):
+            lanes = slice(block * BLOCK, (block + 1) * BLOCK)
+            turned = (table(6)[:, lanes], table(7)[:, lanes])
+            for turn in range(step):
+                row = here * step + turn
+                twist = times((table(4, row, 1)[:, lanes], table(5, row, 1)[:, lanes]), turned)
+                low = pl.ds(turn, sub, stride=step)
+                high = pl.ds(rows + turn, sub, stride=step)
                 value = (
-                    wr[block, low, :] - wi[block, high, :],
-                    wi[block, low, :] + wr[block, high, :],
+                    wr[seg, block, low, :] - wi[seg, block, high, :],
+                    wi[seg, block, low, :] + wr[seg, block, high, :],
                 )
                 real, imag = times(value, twist)
                 out[seg, turn, 0, :, lanes] = real.astype(jnp.bfloat16)
                 out[seg, turn, 1, :, lanes] = imag.astype(jnp.bfloat16)
 
 
-def first_stage(samples, here, columns, size_one, scale):
+def first_tables(samples, ranks):
+    _, _, rows, length = samples.shape
+    columns = np.arange(length) - BLOCK // 2
+    size = rows * ranks * length
+    scale = np.float32(1.0 / math.sqrt(size))
+    coarse = phases(np.arange(length // GROUP)[:, None] * GROUP * columns[None], length)
+    fine = phases(np.arange(GROUP)[:, None] * columns[None], length)
+    outer = np.arange(ranks)[:, None] * rows + np.arange(ranks)[None]
+    outer = [scale * part for part in phases(outer.reshape(-1, 1) * columns[None], size)]
+    inner = phases(np.arange(rows // ranks)[:, None] * ranks * columns[None], size)
+    parts = [*coarse, *fine, *outer, *inner]
+    return tuple(part.shape[0] for part in parts), np.concatenate(parts, 0)
+
+
+def first_stage(samples, heights, tables, ranks, begin, cols):
     segs, comps, rows, length = samples.shape
-    ranks = size_one // rows
-    cols = columns.size
-    coarse_table = phases(np.arange(length // GROUP)[:, None] * GROUP * columns[None], length)
-    fine_table = phases(np.arange(GROUP)[:, None] * columns[None], length)
-    outer = np.arange(ranks)[:, None, None] * rows + np.arange(ranks)[None, :, None]
-    outer = [
-        table * np.float32(scale)
-        for table in phases(outer * columns[None, None], size_one * length)
-    ]
     sub = rows // ranks
-    inner = phases(np.arange(sub)[:, None] * ranks * columns[None], size_one * length)
     return pl.pallas_call(
-        first_kernel,
+        functools.partial(first_kernel, begin, heights),
         out_shape=jax.ShapeDtypeStruct((segs, ranks, comps, sub, cols), jnp.bfloat16),
-        in_specs=[smem()] + [vmem()] * 9,
+        in_specs=[pl.BlockSpec(memory_space=pl.ANY)] * 2,
         out_specs=vmem(),
-        scratch_shapes=[pltpu.VMEM((length, cols), jnp.bfloat16)] * 2
-        + [pltpu.VMEM((cols // BLOCK, segs * comps * rows, BLOCK), jnp.float32)] * 2,
+        scratch_shapes=[
+            pltpu.VMEM(samples.shape, samples.dtype),
+            pltpu.VMEM((tables.shape[0], cols), tables.dtype),
+        ]
+        + [pltpu.VMEM((length, cols), jnp.bfloat16)] * 2
+        + [pltpu.VMEM((segs, cols // BLOCK, comps * rows, BLOCK), jnp.float32)] * 2
+        + [pltpu.SemaphoreType.DMA((segs + 1,))],
         compiler_params=pltpu.CompilerParams(vmem_limit_bytes=FIRST_LIMIT),
         cost_estimate=pl.CostEstimate(
             flops=2 * segs * comps * rows * length * 2 * cols,
@@ -238,10 +262,10 @@
             transcendentals=0,
         ),
         name="first_stage",
-    )(here, samples, *coarse_table, *fine_table, *outer, *inner)
-
-
-def gathered(own, tied):
+    )(samples, tables)
+
+
+def gathered(own):
     near = [(i, i ^ PAIR) for i in range(PAIR * LINE)]
     far = [(i, i ^ (2 * PAIR)) for i in range(PAIR * LINE)]
     flip = [(i, i ^ 1) for i in range(PAIR * LINE)]
@@ -258,24 +282,23 @@
     by_far = send(own, far)
     low = by_near[:half]
     high = by_flip[half:]
-    low, tied = lax.optimization_barrier((low, tied))
     near_low = send(low, flip)
     near_high = send(high, near)
     far_flip = send(by_far, flip)
     relayed = send(by_far, ends)
-    by_cross = crossed + relayed
-    cross_flip = send(by_cross, flip)
+    flip_middle = send(crossed, [pair for pair in flip if pair[0] in dict(middle)])
+    flip_ends = send(relayed, [pair for pair in flip if pair[0] not in dict(middle)])
     return [
-        (0, own, 0),
-        (1, by_flip, 0),
-        (PAIR, by_near, 0),
-        (PAIR + 1, near_low, 0),
-        (PAIR + 1, near_high, half),
-        (2 * PAIR, by_far, 0),
-        (2 * PAIR + 1, far_flip, 0),
-        (3 * PAIR, by_cross, 0),
-        (3 * PAIR + 1, cross_flip, 0),
-    ], tied
+        (0, 0, own),
+        (1, 0, by_flip),
+        (PAIR, 0, by_near),
+        (PAIR + 1, 0, near_low),
+        (PAIR + 1, half, near_high),
+        (2 * PAIR, 0, by_far),
+        (2 * PAIR + 1, 0, far_flip),
+        (3 * PAIR, 0, crossed, relayed),
+        (3 * PAIR + 1, 0, flip_middle, flip_ends),
+    ]
 
 
 def eight(z):
@@ -312,7 +335,7 @@
     planes = segs * kinds
     refs = list(refs)
     ints, weight = refs.pop(0), refs.pop(0)
-    slots = [refs.pop(0) for _ in pieces]
+    slots = [[refs.pop(0) for _ in range(many)] for _, _, many in pieces]
     mats, bands = refs.pop(0), refs.pop(0)
     before = None if first else refs.pop(0)
     total_in = None if first else refs.pop(0)
@@ -325,7 +348,7 @@
         after = refs.pop(0)
     parts, mixed, held, power = (refs.pop(0) for _ in range(4))
     if last:
-        total, theirs = refs.pop(0), refs.pop(0)
+        total = refs.pop(0)
 
     def row_start(plane):
         return ints[2 + plane]
@@ -336,12 +359,15 @@
     def lane_start(plane):
         return ints[2 + 2 * planes + plane]
 
-    for number, (distance, start, length) in enumerate(pieces):
+    for (distance, start, _), arrays in zip(pieces, slots):
         place = lax.bitwise_xor(ints[0], distance)
-        for seg in range(length):
+        for seg in range(arrays[0].shape[0]):
             for turn in range(parts.shape[1]):
                 for comp in range(parts.shape[2]):
-                    parts[start + seg, turn, comp, place] = slots[number][seg, turn, comp]
+                    value = arrays[0][seg, turn, comp]
+                    for other in arrays[1:]:
+                        value = value + other[seg, turn, comp]
+                    parts[start + seg, turn, comp, place] = value
     _, step, comps, ranks, sub, cols = parts.shape
     rows = ranks * sub
     count = cols // BLOCK
@@ -402,22 +428,25 @@
             jnp.concatenate([real_band, imag_band], 1),
             jnp.concatenate([-imag_band, real_band], 1),
         )
-        value = None
-        for comp in range(2):
-            lines = []
-            for seg in range(segs):
-                at = pl.ds(pl.multiple_of(row_start(seg * kinds + kind), SUB), window)
-                for block, _ in outs:
-                    lines.append(
-                        jnp.concatenate(
-                            [row_block(block, seg, comp, at), row_block(block + 1, seg, comp, at)],
-                            1,
-                        )
+        lines = []
+        for seg in range(segs):
+            at = pl.ds(pl.multiple_of(row_start(seg * kinds + kind), SUB), window)
+            for block, _ in outs:
+                lines.append(
+                    jnp.concatenate(
+                        [
+                            row_block(block + side, seg, comp, at)
+                            for comp in range(2)
+                            for side in range(2)
+                        ],
+                        1,
                     )
-            one = jnp.dot(
-                jnp.concatenate(lines, 0), table[comp], preferred_element_type=jnp.float32
-            )
-            value = one if value is None else value + one
+                )
+        value = jnp.dot(
+            jnp.concatenate(lines, 0),
+            jnp.concatenate(table, 0),
+            preferred_element_type=jnp.float32,
+        )
         value = value[:, :BLOCK] ** 2 + value[:, BLOCK:] ** 2
         number = 0
         for seg in range(segs):
@@ -434,17 +463,44 @@
         owned = kinds // 2
         theirs_at = owned * (1 - ints[1])
         mine_at = owned * ints[1]
-        for target, base in ((theirs, theirs_at), (mine_out, mine_at)):
-            for kind in range(owned):
-                for place in range(ranks):
-                    at = pl.ds(place * owned + kind, rows, stride=ranks * owned)
-                    target[at, :] = total[base + kind, place]
-            if target is theirs:
-                send_out[...] = theirs[...].astype(jnp.bfloat16)
+        lane_rows = 8
+        for target, base in ((send_out, theirs_at), (mine_out, mine_at)):
+            for row in range(0, rows, lane_rows):
+                tiles = [
+                    total[base + kind, place, row : row + lane_rows, :]
+                    for place in range(ranks)
+                    for kind in range(owned)
+                ]
+                value = jnp.swapaxes(jnp.stack(tiles, 0), 0, 1).reshape(-1, BLOCK)
+                height = value.shape[0]
+                at = row // lane_rows * height
+                target[at : at + height, :] = value.astype(target.dtype)
+
+
+def bands_kernel(kernels, out):
+    comps, kinds, width = kernels.shape
+    for comp in range(comps):
+        for kind in range(kinds):
+            row = kernels[comp, kind : kind + 1, :].astype(jnp.float32)
+            rows = jnp.broadcast_to(jnp.concatenate([row, jnp.zeros_like(row)], 1), (width, 2 * width))
+            moved = pltpu.roll(rows, 0, 1, stride=1, stride_axis=0)
+            out[comp, kind] = moved.T.astype(jnp.bfloat16)
+
+
+def banded(kernels):
+    comps, kinds, width = kernels.shape
+    return pl.pallas_call(
+        bands_kernel,
+        out_shape=jax.ShapeDtypeStruct((comps, kinds, 2 * width, width), kernels.dtype),
+        in_specs=[vmem()],
+        out_specs=vmem(),
+        compiler_params=pltpu.CompilerParams(vmem_limit_bytes=FIRST_LIMIT),
+        name="banded",
+    )(kernels)
 
 
 def chunk(scalars, slots, tables, carried, residues, first, last):
-    own = slots[0][1]
+    own = slots[0][2]
     segs, step, comps, sub, cols = own.shape
     ranks = step
     rows = ranks * sub
@@ -470,9 +526,9 @@
         out_shape = [total, edge]
     if first:
         out_shape.append(edge)
-    pieces = tuple((distance, begin, piece.shape[0]) for distance, piece, begin in slots)
+    pieces = tuple((slot[0], slot[1], len(slot) - 2) for slot in slots)
     plan = (pieces, first, last, tuple(outs), segs, kinds)
-    arrays = [piece for _, piece, _ in slots]
+    arrays = [array for slot in slots for array in slot[2:]]
     inputs = [*scalars, *arrays, mats, bands, *carried]
     specs = [smem()] * 2 + [vmem()] * (len(inputs) - 2)
     scratch = [
@@ -482,7 +538,7 @@
         pltpu.VMEM((2, segs * len(outs), window, BLOCK), jnp.float32),
     ]
     if last:
-        scratch += [pltpu.VMEM(total.shape, total.dtype), pltpu.VMEM(flat, jnp.float32)]
+        scratch.append(pltpu.VMEM(total.shape, total.dtype))
     return pl.pallas_call(
         functools.partial(chunk_kernel, plan),
         out_shape=out_shape,
@@ -508,17 +564,14 @@
     kinds = kernels.shape[1]
     blocks_here = length // ranks // BLOCK
     places = jnp.stack([lax.axis_index("freq"), lax.axis_index("seg")]).astype(jnp.int32)
-    columns = np.arange(cols_two) - BLOCK // 2
     groups = np.split(np.arange(ranks), SPLITS)
+    heights, tables = first_tables(samples, ranks)
+    tables = jnp.asarray(tables)
     turned = []
     for group in groups:
         turned.append(
             first_stage(
-                samples,
-                places,
-                columns[group[0] * BLOCK : (group[-1] + 1) * BLOCK],
-                size_one,
-                1.0 / math.sqrt(length),
+                samples, heights, tables, ranks, group[0] * BLOCK, group.size * BLOCK
             )
         )
 
@@ -527,12 +580,11 @@
     mats = np.concatenate(
         [np.concatenate([real, -imag], 2), np.concatenate([imag, real], 2)], 1
     ).astype(jnp.bfloat16)
-    bands = jnp.swapaxes(toeplitz(kernels), -1, -2)
+    bands = banded(kernels)
 
     slots = []
     for own in turned:
-        pieces, bands = gathered(own, bands)
-        slots.append(pieces)
+        slots.append(gathered(own))
 
     bins = jnp.remainder(
         lax.axis_index("freq") * blocks_here + offsets.reshape(segs * kinds), ranks * blocks_here

time: 170 us -> 139 us (0.82)
  waiting for transfers between devices: 87.6 us -> 65.2 us
  local copies, waits for them, and re-layouts: 16.4 us -> 5.06 us
  starting transfers between devices: 30.2 us -> 39 us
  other arithmetic: 4.85 us -> 1.71 us
    ppermute x18 -> x20, waiting for transfers between devices: 85 us -> 62.5 us  [send(): return lax.ppermute(array, 'freq', route)]
    ppermute x18 -> x20, starting transfers between devices: 30.1 us -> 38.9 us  [send(): return lax.ppermute(array, 'freq', route)]
    another operation x2 -> x0, local copies, waits for them, and re-layouts: 5.13 us -> none  [toeplitz(): tiled = jnp.tile(padded, (1, 1, width))[..., :2 * width * width]]
    pallas_call x2, Pallas kernels: 19.7 us -> 16.2 us  [chunk(): pl.pallas_call(functools.partial(chunk_kernel, plan), out_shape=out_shape...]
    add x2 -> x0, other arithmetic: 2.46 us -> none  [gathered(): by_cross = crossed + relayed]
    pallas_call x2 -> x3, Pallas kernels: 9.18 us -> 11 us  [the longest x2 8.79 us: first_stage(): pl.pallas_call(functools.partial(first_kernel, begin, heights), out_shape...]
    reshape x1 -> x0, local copies, waits for them, and re-layouts: 1.82 us -> none  [toeplitz(): return tiled.reshape(kernels.shape[:-1] + (width, 2 * width))]
    slice x2, local copies, waits for them, and re-layouts: 1.76 us -> 0.04 us  [gathered(): high = by_flip[half:]]
  transfers between devices with their start and end apart: 19 -> 21, of which waited for: 6 -> 5; matrix products, arithmetic and copies ran while one was open for 8% -> 1% of each run, Pallas kernels for 8% -> 10%
where the time goes in v1:
time: 139 us; the launch traced here: 138 us
  waiting for transfers between devices  65.2 us (47%)
  starting transfers between devices  39 us (28%)
  Pallas kernels  27.2 us (20%)
  local copies, waits for them, and re-layouts  5.06 us (4%)
  other arithmetic  1.71 us (1%)
    ppermute x20, waiting for transfers between devices, send(): return lax.ppermute(array, 'freq', route)  62.5 us
    ppermute x20, starting transfers between devices, send(): return lax.ppermute(array, 'freq', route)  38.9 us
    pallas_call x2, Pallas kernels, chunk(): pl.pallas_call(functools.partial(chunk_kernel, plan), out_shape=out_shape...  16.2 us
    pallas_call x2, Pallas kernels, first_stage(): pl.pallas_call(functools.partial(first_kernel, begin, heights), out_shape...  8.79 us
    unnamed x22, local copies, waits for them, and re-layouts  4.12 us
  transfers between devices with their start and end apart: 21, of which 5 were waited for; matrix products, arithmetic and copies ran while one was open for 1% of the time, Pallas kernels for 10%

profile of v1, /device:TPU:0, one launch (start us, length us, event | category | flops | bytes accessed | tf_op | source)
XLA Modules:
  0.0 138.4 jit_solution(5702991296919681548)
XLA Ops:
  0.0 4.4 %first_stage.3.refs_2_ = bf16[2,8,2,16,512]{4,3,2,1,0:T(8,128)(2,1)} custom-call(f32[2,2,128,1024]{3,2,1,0:T(8,128)} %x_hbm.3, f32[288,1024]{1,0:T(8,128)} %constant.63.clone.tables_hbm), custom_call_target="tpu_custom_call" | custom-call | flops 1073741824 | bytes 2097152 | tf_op jit(solution)/shard_map/first_stage/pallas_call | solution.py:246
  4.4 0.0 copy-start.8
  4.4 0.0 copy-start.9
  4.4 0.0 copy-start.10
  4.4 4.1 %collective-permute-start.14 = (bf16[2,8,2,16,512]{4,3,2,1,0:T(8,128)(2,1)}, bf16[2,8,2,16,512]{4,3,2,1,0:T(8,128)(2,1)}, u32[]{:S(2)}, u32[]{:S(2)}) collective-permute-start(bf16[2,8,2,16,512]{4,3,2,1,0:T(8,128)(2,1)} %first_stage.3.refs_2_), channel_id=1, source_target_pairs={{0,8},{2,10},{4,12},{6,14},{8,0},{10,2},{12,4},{14,6},{1,9},{3,11}... | collective-permute-start | bytes 1572872 | tf_op jit(solution)/shard_map/ppermute | solution.py:277
  8.6 1.6 %collective-permute-start.11 = (bf16[2,8,2,16,512]{4,3,2,1,0:T(8,128)(2,1)}, bf16[2,8,2,16,512]{4,3,2,1,0:T(8,128)(2,1)S(1)}, u32[]{:S(2)}, u32[]{:S(2)}) collective-permute-start(bf16[2,8,2,16,512]{4,3,2,1,0:T(8,128)(2,1)} %first_stage.3.refs_2_), channel_id=1, source_target_pairs={{0,4},{2,6},{4,0},{6,2},{8,12},{10,14},{12,8},{14,10},{1,5},{3,7},... | collective-permute-start | bytes 1572872 | tf_op jit(solution)/shard_map/ppermute | solution.py:277
  10.1 1.5 %collective-permute-start.10 = (bf16[2,8,2,16,512]{4,3,2,1,0:T(8,128)(2,1)}, bf16[2,8,2,16,512]{4,3,2,1,0:T(8,128)(2,1)S(1)}, u32[]{:S(2)}, u32[]{:S(2)}) collective-permute-start(bf16[2,8,2,16,512]{4,3,2,1,0:T(8,128)(2,1)} %first_stage.3.refs_2_), channel_id=1, source_target_pairs={{0,2},{2,0},{4,6},{6,4},{8,10},{10,8},{12,14},{14,12},{1,3},{3,1},... | collective-permute-start | bytes 1572872 | tf_op jit(solution)/shard_map/ppermute | solution.py:277
  11.6 1.5 %collective-permute-start.16 = (bf16[2,8,2,16,512]{4,3,2,1,0:T(8,128)(2,1)}, bf16[2,8,2,16,512]{4,3,2,1,0:T(8,128)(2,1)}, u32[]{:S(2)}, u32[]{:S(2)}) collective-permute-start(bf16[2,8,2,16,512]{4,3,2,1,0:T(8,128)(2,1)} %first_stage.3.refs_2_), channel_id=1, source_target_pairs={{4,8},{6,10},{8,4},{10,6},{5,9},{7,11},{9,5},{11,7},{20,24},{22,26... | collective-permute-start | bytes 1572872 | tf_op jit(solution)/shard_map/ppermute | solution.py:277
  13.1 4.4 %first_stage.2.refs_2_ = bf16[2,8,2,16,512]{4,3,2,1,0:T(8,128)(2,1)} custom-call(f32[2,2,128,1024]{3,2,1,0:T(8,128)} %x_hbm.3, f32[288,1024]{1,0:T(8,128)} %constant.63.clone.tables_hbm), custom_call_target="tpu_custom_call" | custom-call | flops 1073741824 | bytes 2097152 | tf_op jit(solution)/shard_map/first_stage/pallas_call | solution.py:246
  17.5 2.4 %collective-permute-start.4 = (bf16[2,8,2,16,512]{4,3,2,1,0:T(8,128)(2,1)}, bf16[2,8,2,16,512]{4,3,2,1,0:T(8,128)(2,1)S(1)}, u32[]{:S(2)}, u32[]{:S(2)}) collective-permute-start(bf16[2,8,2,16,512]{4,3,2,1,0:T(8,128)(2,1)} %first_stage.2.refs_2_), channel_id=1, source_target_pairs={{0,8},{2,10},{4,12},{6,14},{8,0},{10,2},{12,4},{14,6},{1,9},{3,11}... | collective-permute-start | bytes 1572872 | tf_op jit(solution)/shard_map/ppermute | solution.py:277
  19.9 13.9 %collective-permute-done.14.refs_7_ = bf16[2,8,2,16,512]{4,3,2,1,0:T(8,128)(2,1)} collective-permute-done((bf16[2,8,2,16,512]{4,3,2,1,0:T(8,128)(2,1)}, bf16[2,8,2,16,512]{4,3,2,1,0:T(8,128)(2,1)}, u32[]{:S(2)}, u32[]{:S(2)}) %collective-permute-start.14) | collective-permute-done | bytes 524320 | tf_op jit(solution)/shard_map/ppermute | solution.py:277
  33.8 0.0 collective-permute-start.1
  33.8 0.0 collective-permute-done.11.refs_4_
  33.8 2.0 %collective-permute-start = (bf16[2,8,2,16,512]{4,3,2,1,0:T(8,128)(2,1)}, bf16[2,8,2,16,512]{4,3,2,1,0:T(8,128)(2,1)S(1)}, u32[]{:S(2)}, u32[]{:S(2)}) collective-permute-start(bf16[2,8,2,16,512]{4,3,2,1,0:T(8,128)(2,1)} %first_stage.2.refs_2_), channel_id=1, source_target_pairs={{0,2},{2,0},{4,6},{6,4},{8,10},{10,8},{12,14},{14,12},{1,3},{3,1},... | collective-permute-start | bytes 1572872 | tf_op jit(solution)/shard_map/ppermute | solution.py:277
  35.8 0.0 collective-permute-done.10.refs_3_
  35.8 1.5 %collective-permute-start.6 = (bf16[2,8,2,16,512]{4,3,2,1,0:T(8,128)(2,1)}, bf16[2,8,2,16,512]{4,3,2,1,0:T(8,128)(2,1)}, u32[]{:S(2)}, u32[]{:S(2)}) collective-permute-start(bf16[2,8,2,16,512]{4,3,2,1,0:T(8,128)(2,1)} %first_stage.2.refs_2_), channel_id=1, source_target_pairs={{4,8},{6,10},{8,4},{10,6},{5,9},{7,11},{9,5},{11,7},{20,24},{22,26... | collective-permute-start | bytes 1572872 | tf_op jit(solution)/shard_map/ppermute | solution.py:277
  37.3 0.0 collective-permute-done.16.refs_9_
  37.3 1.3 collective-permute-start.17
  38.6 0.7 slice.18
  39.3 27.3 %collective-permute-done.4.refs_7_ = bf16[2,8,2,16,512]{4,3,2,1,0:T(8,128)(2,1)S(1)} collective-permute-done((bf16[2,8,2,16,512]{4,3,2,1,0:T(8,128)(2,1)}, bf16[2,8,2,16,512]{4,3,2,1,0:T(8,128)(2,1)S(1)}, u32[]{:S(2)}, u32[]{:S(2)}) %collective-permute-start.4) | collective-permute-done | bytes 524320 | tf_op jit(solution)/shard_map/ppermute | solution.py:277
  66.6 1.8 %collective-permute-start.12 = (bf16[1,8,2,16,512]{4,3,2,1,0:T(8,128)(2,1)}, bf16[1,8,2,16,512]{4,3,2,1,0:T(8,128)(2,1)S(1)}, u32[]{:S(2)}, u32[]{:S(2)}) collective-permute-start(bf16[1,8,2,16,512]{4,3,2,1,0:T(8,128)(2,1)} %slice.18), channel_id=1, source_target_pairs={{0,2},{2,0},{4,6},{6,4},{8,10},{10,8},{12,14},{14,12},{1,3},{3,1},... | collective-permute-start | bytes 786440 | tf_op jit(solution)/shard_map/ppermute | solution.py:277
  68.4 0.0 collective-permute-done.1.refs_4_
  68.4 0.2 collective-permute-start.15
  68.6 1.3 collective-permute-start.7
  69.9 0.1 add.22
  70.0 0.0 collective-permute-done.6.refs_9_
  70.0 7.7 %collective-permute-start.13 = (bf16[1,8,2,16,512]{4,3,2,1,0:T(8,128)(2,1)S(1)}, bf16[1,8,2,16,512]{4,3,2,1,0:T(8,128)(2,1)S(1)}, u32[]{:S(2)}, u32[]{:S(2)}) collective-permute-start(bf16[1,8,2,16,512]{4,3,2,1,0:T(8,128)(2,1)S(1)} %slice.19), channel_id=1, source_target_pairs={{0,4},{2,6},{4,0},{6,2},{8,12},{10,14},{12,8},{14,10},{1,5},{3,7},... | collective-permute-start | bytes 786440 | tf_op jit(solution)/shard_map/ppermute | solution.py:277
  77.8 1.5 %collective-permute-start.18 = (bf16[2,8,2,16,512]{4,3,2,1,0:T(8,128)(2,1)}, bf16[2,8,2,16,512]{4,3,2,1,0:T(8,128)(2,1)}, u32[]{:S(2)}, u32[]{:S(2)}) collective-permute-start(bf16[2,8,2,16,512]{4,3,2,1,0:T(8,128)(2,1)} %collective-permute-done.16.refs_9_), channel_id=1, source_target_pairs={{4,6},{6,4},{8,10},{10,8},{5,7},{7,5},{9,11},{11,9},{20,22},{22,20... | collective-permute-start | bytes 1572872 | tf_op jit(solution)/shard_map/ppermute | solution.py:277
  79.2 3.4 %collective-permute-start.19 = (bf16[2,8,2,16,512]{4,3,2,1,0:T(8,128)(2,1)}, bf16[2,8,2,16,512]{4,3,2,1,0:T(8,128)(2,1)}, u32[]{:S(2)}, u32[]{:S(2)}) collective-permute-start(bf16[2,8,2,16,512]{4,3,2,1,0:T(8,128)(2,1)} %collective-permute-done.17.refs_10_), channel_id=1, source_target_pairs={{0,2},{2,0},{12,14},{14,12},{1,3},{3,1},{13,15},{15,13},{16,18},{1... | collective-permute-start | bytes 1572872 | tf_op jit(solution)/shard_map/ppermute | solution.py:277
  82.7 11.1 %collective-permute-done.13.refs_6_ = bf16[1,8,2,16,512]{4,3,2,1,0:T(8,128)(2,1)S(1)} collective-permute-done((bf16[1,8,2,16,512]{4,3,2,1,0:T(8,128)(2,1)S(1)}, bf16[1,8,2,16,512]{4,3,2,1,0:T(8,128)(2,1)S(1)}, u32[]{:S(2)}, u32[]{:S(2)}) %collective-permute-start.13) | collective-permute-done | bytes 262176 | tf_op jit(solution)/shard_map/ppermute | solution.py:277
  93.8 0.7 copy-done.4
  94.5 1.5 %collective-permute-start.5 = (bf16[2,8,2,16,512]{4,3,2,1,0:T(8,128)(2,1)S(1)}, bf16[2,8,2,16,512]{4,3,2,1,0:T(8,128)(2,1)}, u32[]{:S(2)}, u32[]{:S(2)}) collective-permute-start(bf16[2,8,2,16,512]{4,3,2,1,0:T(8,128)(2,1)S(1)} %collective-permute-done.4.refs_7_), channel_id=1, source_target_pairs={{0,2},{2,0},{4,6},{6,4},{8,10},{10,8},{12,14},{14,12},{1,3},{3,1},... | collective-permute-start | bytes 1572872 | tf_op jit(solution)/shard_map/ppermute | solution.py:277
  96.0 1.5 %collective-permute-start.8 = (bf16[2,8,2,16,512]{4,3,2,1,0:T(8,128)(2,1)}, bf16[2,8,2,16,512]{4,3,2,1,0:T(8,128)(2,1)}, u32[]{:S(2)}, u32[]{:S(2)}) collective-permute-start(bf16[2,8,2,16,512]{4,3,2,1,0:T(8,128)(2,1)} %collective-permute-done.6.refs_9_), channel_id=1, source_target_pairs={{4,6},{6,4},{8,10},{10,8},{5,7},{7,5},{9,11},{11,9},{20,22},{22,20... | collective-permute-start | bytes 1572872 | tf_op jit(solution)/shard_map/ppermute | solution.py:277
  97.5 2.6 %collective-permute-start.9 = (bf16[2,8,2,16,512]{4,3,2,1,0:T(8,128)(2,1)}, bf16[2,8,2,16,512]{4,3,2,1,0:T(8,128)(2,1)}, u32[]{:S(2)}, u32[]{:S(2)}) collective-permute-start(bf16[2,8,2,16,512]{4,3,2,1,0:T(8,128)(2,1)} %collective-permute-done.7.refs_10_), channel_id=1, source_target_pairs={{0,2},{2,0},{12,14},{14,12},{1,3},{3,1},{13,15},{15,13},{16,18},{1... | collective-permute-start | bytes 1572872 | tf_op jit(solution)/shard_map/ppermute | solution.py:277
  100.1 0.2 fusion
  100.2 2.2 %banded.1.refs_14_ = bf16[2,8,256,128]{3,2,1,0:T(8,128)(2,1)} custom-call(bf16[2,8,128]{2,1,0:T(8,128)(2,1)} %kernels.1), custom_call_target="tpu_custom_call" | custom-call | tf_op jit(solution)/shard_map/banded/pallas_call | solution.py:492
  102.5 0.1 concatenate.3.refs_0_
  102.6 1.6 %collective-permute-start.2 = (bf16[1,8,2,16,512]{4,3,2,1,0:T(8,128)(2,1)S(1)}, bf16[1,8,2,16,512]{4,3,2,1,0:T(8,128)(2,1)S(1)}, u32[]{:S(2)}, u32[]{:S(2)}) collective-permute-start(bf16[1,8,2,16,512]{4,3,2,1,0:T(8,128)(2,1)S(1)} %slice.16), channel_id=1, source_target_pairs={{0,2},{2,0},{4,6},{6,4},{8,10},{10,8},{12,14},{14,12},{1,3},{3,1},... | collective-permute-start | bytes 786440 | tf_op jit(solution)/shard_map/ppermute | solution.py:277
  104.3 0.0 copy-start
  104.3 1.2 copy-done
  105.5 0.9 copy-done.5
  106.4 1.2 copy-done.6
  107.7 7.3 %chunk.2 = (f32[8,8,128,128]{3,2,1,0:T(8,128)S(1)}, bf16[2,2,1152,128]{3,2,1,0:T(8,128)(2,1)S(1)}, bf16[2,2,1152,128]{3,2,1,0:T(8,128)(2,1)S(1)}) custom-call(s32[50]{0:T(128)S(1)} %concatenate.3.refs_0_, f32[2]{0:T(128)S(1)} %broadcast_multiply_fusion.refs_1_, bf16[2,8,2,16,512]{4,3,2,1,0:T(8,128)(2,1)S(1)} %copy-done.3, ...), custom_call_target="tpu_custom_call" | custom-call | flops 2885681152 | bytes 8388608 | tf_op jit(solution)/shard_map/chunk/pallas_call | solution.py:542
  115.0 10.3 %collective-permute-done.2.refs_5_ = bf16[1,8,2,16,512]{4,3,2,1,0:T(8,128)(2,1)S(1)} collective-permute-done((bf16[1,8,2,16,512]{4,3,2,1,0:T(8,128)(2,1)S(1)}, bf16[1,8,2,16,512]{4,3,2,1,0:T(8,128)(2,1)S(1)}, u32[]{:S(2)}, u32[]{:S(2)}) %collective-permute-start.2) | collective-permute-done | bytes 262176 | tf_op jit(solution)/shard_map/ppermute | solution.py:277
  125.3 8.8 %chunk.3 = (f32[4096,128]{1,0:T(8,128)S(1)}, bf16[4096,128]{1,0:T(8,128)(2,1)S(1)}) custom-call(s32[50]{0:T(128)S(1)} %concatenate.3.refs_0_, f32[2]{0:T(128)S(1)} %broadcast_multiply_fusion.refs_1_, bf16[2,8,2,16,512]{4,3,2,1,0:T(8,128)(2,1)S(1)} %copy-done.2, bf16[2,8,2,16,512]{4,3,2,1,0:T(8,128)(2,1)S(1)} %collective-permute-done.refs_3_, ...), custom_call_target="tpu_custom_call" | custom-call | flops 4093640704 | bytes 8388608 | tf_op jit(solution)/shard_map/chunk/pallas_call | solution.py:542
  134.2 0.1 collective-permute-start.20
  134.2 2.6 %collective-permute-done.20 = bf16[4096,128]{1,0:T(8,128)(2,1)S(1)} collective-permute-done((bf16[4096,128]{1,0:T(8,128)(2,1)S(1)}, bf16[4096,128]{1,0:T(8,128)(2,1)S(1)}, u32[]{:S(2)}, u32[]{:S(2)}) %collective-permute-start.20) | collective-permute-done | bytes 1048608 | tf_op jit(solution)/shard_map/ppermute | solution.py:615
  136.9 1.5 %convert_add_fusion = f32[4096,128]{1,0:T(8,128)} fusion(f32[4096,128]{1,0:T(8,128)S(1)} %get-tuple-element.13, bf16[4096,128]{1,0:T(8,128)(2,1)S(1)} %collective-permute-done.20), kind=kLoop, calls=%fused_computation | loop fusion | flops 1048576 | bytes 5242880 | tf_op jit(solution)/shard_map/add | solution.py:616
  (33 shorter events, 0.2 us)
Async XLA Ops:
  4.4 65.5 %copy-start.8 = (s32[2,8]{1,0:T(2,128)S(1)}, s32[2,8]{1,0:T(2,128)}, u32[]{:S(2)}) copy-start(s32[2,8]{1,0:T(2,128)} %param.9) | copy-start | bytes 196
  4.4 95.6 %copy-start.9 = (f32[16]{0:T(128)S(1)}, f32[16]{0:T(128)}, u32[]{:S(2)}) copy-start(f32[16]{0:T(128)} %param.11) | copy-start | bytes 196
  4.4 95.6 %copy-start.10 = (s32[2]{0:T(128)S(1)}, s32[2]{0:T(128)}, u32[]{:S(2)}) copy-start(s32[2]{0:T(128)} %param.10) | copy-start | bytes 28
  4.4 29.4 %collective-permute-start.14 = (bf16[2,8,2,16,512]{4,3,2,1,0:T(8,128)(2,1)}, bf16[2,8,2,16,512]{4,3,2,1,0:T(8,128)(2,1)}, u32[]{:S(2)}, u32[]{:S(2)}) collective-permute-start(bf16[2,8,2,16,512]{4,3,2,1,0:T(8,128)(2,1)} %first_stage.3.refs_2_), channel_id=1, source_target_pairs={{0,8},{2,10},{4,12},{6,14},{8,0},{10,2},{12,4},{14,6},{1,9},{3,11}... | collective-permute-start | bytes 1572872 | tf_op jit(solution)/shard_map/ppermute | solution.py:277
  8.6 25.2 %collective-permute-start.11 = (bf16[2,8,2,16,512]{4,3,2,1,0:T(8,128)(2,1)}, bf16[2,8,2,16,512]{4,3,2,1,0:T(8,128)(2,1)S(1)}, u32[]{:S(2)}, u32[]{:S(2)}) collective-permute-start(bf16[2,8,2,16,512]{4,3,2,1,0:T(8,128)(2,1)} %first_stage.3.refs_2_), channel_id=1, source_target_pairs={{0,4},{2,6},{4,0},{6,2},{8,12},{10,14},{12,8},{14,10},{1,5},{3,7},... | collective-permute-start | bytes 1572872 | tf_op jit(solution)/shard_map/ppermute | solution.py:277
  10.1 25.7 %collective-permute-start.10 = (bf16[2,8,2,16,512]{4,3,2,1,0:T(8,128)(2,1)}, bf16[2,8,2,16,512]{4,3,2,1,0:T(8,128)(2,1)S(1)}, u32[]{:S(2)}, u32[]{:S(2)}) collective-permute-start(bf16[2,8,2,16,512]{4,3,2,1,0:T(8,128)(2,1)} %first_stage.3.refs_2_), channel_id=1, source_target_pairs={{0,2},{2,0},{4,6},{6,4},{8,10},{10,8},{12,14},{14,12},{1,3},{3,1},... | collective-permute-start | bytes 1572872 | tf_op jit(solution)/shard_map/ppermute | solution.py:277
  11.6 25.7 %collective-permute-start.16 = (bf16[2,8,2,16,512]{4,3,2,1,0:T(8,128)(2,1)}, bf16[2,8,2,16,512]{4,3,2,1,0:T(8,128)(2,1)}, u32[]{:S(2)}, u32[]{:S(2)}) collective-permute-start(bf16[2,8,2,16,512]{4,3,2,1,0:T(8,128)(2,1)} %first_stage.3.refs_2_), channel_id=1, source_target_pairs={{4,8},{6,10},{8,4},{10,6},{5,9},{7,11},{9,5},{11,7},{20,24},{22,26... | collective-permute-start | bytes 1572872 | tf_op jit(solution)/shard_map/ppermute | solution.py:277
  17.5 86.8 %copy-start.3 = (bf16[2,8,2,16,512]{4,3,2,1,0:T(8,128)(2,1)S(1)}, bf16[2,8,2,16,512]{4,3,2,1,0:T(8,128)(2,1)}, u32[]{:S(2)}) copy-start(bf16[2,8,2,16,512]{4,3,2,1,0:T(8,128)(2,1)} %first_stage.3.refs_2_) | copy-start | bytes 1572868
  17.5 49.1 %collective-permute-start.4 = (bf16[2,8,2,16,512]{4,3,2,1,0:T(8,128)(2,1)}, bf16[2,8,2,16,512]{4,3,2,1,0:T(8,128)(2,1)S(1)}, u32[]{:S(2)}, u32[]{:S(2)}) collective-permute-start(bf16[2,8,2,16,512]{4,3,2,1,0:T(8,128)(2,1)} %first_stage.2.refs_2_), channel_id=1, source_target_pairs={{0,8},{2,10},{4,12},{6,14},{8,0},{10,2},{12,4},{14,6},{1,9},{3,11}... | collective-permute-start | bytes 1572872 | tf_op jit(solution)/shard_map/ppermute | solution.py:277
  33.8 34.6 %collective-permute-start.1 = (bf16[2,8,2,16,512]{4,3,2,1,0:T(8,128)(2,1)}, bf16[2,8,2,16,512]{4,3,2,1,0:T(8,128)(2,1)S(1)}, u32[]{:S(2)}, u32[]{:S(2)}) collective-permute-start(bf16[2,8,2,16,512]{4,3,2,1,0:T(8,128)(2,1)} %first_stage.2.refs_2_), channel_id=1, source_target_pairs={{0,4},{2,6},{4,0},{6,2},{8,12},{10,14},{12,8},{14,10},{1,5},{3,7},... | collective-permute-start | bytes 1572872 | tf_op jit(solution)/shard_map/ppermute | solution.py:277
  33.8 34.8 %collective-permute-start = (bf16[2,8,2,16,512]{4,3,2,1,0:T(8,128)(2,1)}, bf16[2,8,2,16,512]{4,3,2,1,0:T(8,128)(2,1)S(1)}, u32[]{:S(2)}, u32[]{:S(2)}) collective-permute-start(bf16[2,8,2,16,512]{4,3,2,1,0:T(8,128)(2,1)} %first_stage.2.refs_2_), channel_id=1, source_target_pairs={{0,2},{2,0},{4,6},{6,4},{8,10},{10,8},{12,14},{14,12},{1,3},{3,1},... | collective-permute-start | bytes 1572872 | tf_op jit(solution)/shard_map/ppermute | solution.py:277
  35.8 34.2 %collective-permute-start.6 = (bf16[2,8,2,16,512]{4,3,2,1,0:T(8,128)(2,1)}, bf16[2,8,2,16,512]{4,3,2,1,0:T(8,128)(2,1)}, u32[]{:S(2)}, u32[]{:S(2)}) collective-permute-start(bf16[2,8,2,16,512]{4,3,2,1,0:T(8,128)(2,1)} %first_stage.2.refs_2_), channel_id=1, source_target_pairs={{4,8},{6,10},{8,4},{10,6},{5,9},{7,11},{9,5},{11,7},{20,24},{22,26... | collective-permute-start | bytes 1572872 | tf_op jit(solution)/shard_map/ppermute | solution.py:277
  37.3 41.9 %collective-permute-start.17 = (bf16[2,8,2,16,512]{4,3,2,1,0:T(8,128)(2,1)}, bf16[2,8,2,16,512]{4,3,2,1,0:T(8,128)(2,1)}, u32[]{:S(2)}, u32[]{:S(2)}) collective-permute-start(bf16[2,8,2,16,512]{4,3,2,1,0:T(8,128)(2,1)} %collective-permute-done.14.refs_7_), channel_id=1, source_target_pairs={{4,0},{6,2},{8,12},{10,14},{5,1},{7,3},{9,13},{11,15},{20,16},{22,... | collective-permute-start | bytes 1572872 | tf_op jit(solution)/shard_map/ppermute | solution.py:277
  66.6 11.2 %collective-permute-start.12 = (bf16[1,8,2,16,512]{4,3,2,1,0:T(8,128)(2,1)}, bf16[1,8,2,16,512]{4,3,2,1,0:T(8,128)(2,1)S(1)}, u32[]{:S(2)}, u32[]{:S(2)}) collective-permute-start(bf16[1,8,2,16,512]{4,3,2,1,0:T(8,128)(2,1)} %slice.18), channel_id=1, source_target_pairs={{0,2},{2,0},{4,6},{6,4},{8,10},{10,8},{12,14},{14,12},{1,3},{3,1},... | collective-permute-start | bytes 786440 | tf_op jit(solution)/shard_map/ppermute | solution.py:277
  68.4 27.6 %collective-permute-start.15 = (bf16[2,8,2,16,512]{4,3,2,1,0:T(8,128)(2,1)}, bf16[2,8,2,16,512]{4,3,2,1,0:T(8,128)(2,1)}, u32[]{:S(2)}, u32[]{:S(2)}) collective-permute-start(bf16[2,8,2,16,512]{4,3,2,1,0:T(8,128)(2,1)} %collective-permute-done.14.refs_7_), channel_id=1, source_target_pairs={{0,2},{2,0},{4,6},{6,4},{8,10},{10,8},{12,14},{14,12},{1,3},{3,1},... | collective-permute-start | bytes 1572872 | tf_op jit(solution)/shard_map/ppermute | solution.py:277
  68.6 28.9 %collective-permute-start.7 = (bf16[2,8,2,16,512]{4,3,2,1,0:T(8,128)(2,1)S(1)}, bf16[2,8,2,16,512]{4,3,2,1,0:T(8,128)(2,1)}, u32[]{:S(2)}, u32[]{:S(2)}) collective-permute-start(bf16[2,8,2,16,512]{4,3,2,1,0:T(8,128)(2,1)S(1)} %collective-permute-done.4.refs_7_), channel_id=1, source_target_pairs={{4,0},{6,2},{8,12},{10,14},{5,1},{7,3},{9,13},{11,15},{20,16},{22,... | collective-permute-start | bytes 1572872 | tf_op jit(solution)/shard_map/ppermute | solution.py:277
  70.0 23.7 %collective-permute-start.13 = (bf16[1,8,2,16,512]{4,3,2,1,0:T(8,128)(2,1)S(1)}, bf16[1,8,2,16,512]{4,3,2,1,0:T(8,128)(2,1)S(1)}, u32[]{:S(2)}, u32[]{:S(2)}) collective-permute-start(bf16[1,8,2,16,512]{4,3,2,1,0:T(8,128)(2,1)S(1)} %slice.19), channel_id=1, source_target_pairs={{0,4},{2,6},{4,0},{6,2},{8,12},{10,14},{12,8},{14,10},{1,5},{3,7},... | collective-permute-start | bytes 786440 | tf_op jit(solution)/shard_map/ppermute | solution.py:277
  77.8 24.9 %collective-permute-start.18 = (bf16[2,8,2,16,512]{4,3,2,1,0:T(8,128)(2,1)}, bf16[2,8,2,16,512]{4,3,2,1,0:T(8,128)(2,1)}, u32[]{:S(2)}, u32[]{:S(2)}) collective-permute-start(bf16[2,8,2,16,512]{4,3,2,1,0:T(8,128)(2,1)} %collective-permute-done.16.refs_9_), channel_id=1, source_target_pairs={{4,6},{6,4},{8,10},{10,8},{5,7},{7,5},{9,11},{11,9},{20,22},{22,20... | collective-permute-start | bytes 1572872 | tf_op jit(solution)/shard_map/ppermute | solution.py:277
  79.2 25.0 %collective-permute-start.19 = (bf16[2,8,2,16,512]{4,3,2,1,0:T(8,128)(2,1)}, bf16[2,8,2,16,512]{4,3,2,1,0:T(8,128)(2,1)}, u32[]{:S(2)}, u32[]{:S(2)}) collective-permute-start(bf16[2,8,2,16,512]{4,3,2,1,0:T(8,128)(2,1)} %collective-permute-done.17.refs_10_), channel_id=1, source_target_pairs={{0,2},{2,0},{12,14},{14,12},{1,3},{3,1},{13,15},{15,13},{16,18},{1... | collective-permute-start | bytes 1572872 | tf_op jit(solution)/shard_map/ppermute | solution.py:277
  93.8 0.7 copy-start.4
  94.5 30.8 %collective-permute-start.5 = (bf16[2,8,2,16,512]{4,3,2,1,0:T(8,128)(2,1)S(1)}, bf16[2,8,2,16,512]{4,3,2,1,0:T(8,128)(2,1)}, u32[]{:S(2)}, u32[]{:S(2)}) collective-permute-start(bf16[2,8,2,16,512]{4,3,2,1,0:T(8,128)(2,1)S(1)} %collective-permute-done.4.refs_7_), channel_id=1, source_target_pairs={{0,2},{2,0},{4,6},{6,4},{8,10},{10,8},{12,14},{14,12},{1,3},{3,1},... | collective-permute-start | bytes 1572872 | tf_op jit(solution)/shard_map/ppermute | solution.py:277
  96.0 29.3 %collective-permute-start.8 = (bf16[2,8,2,16,512]{4,3,2,1,0:T(8,128)(2,1)}, bf16[2,8,2,16,512]{4,3,2,1,0:T(8,128)(2,1)}, u32[]{:S(2)}, u32[]{:S(2)}) collective-permute-start(bf16[2,8,2,16,512]{4,3,2,1,0:T(8,128)(2,1)} %collective-permute-done.6.refs_9_), channel_id=1, source_target_pairs={{4,6},{6,4},{8,10},{10,8},{5,7},{7,5},{9,11},{11,9},{20,22},{22,20... | collective-permute-start | bytes 1572872 | tf_op jit(solution)/shard_map/ppermute | solution.py:277
  97.5 27.8 %collective-permute-start.9 = (bf16[2,8,2,16,512]{4,3,2,1,0:T(8,128)(2,1)}, bf16[2,8,2,16,512]{4,3,2,1,0:T(8,128)(2,1)}, u32[]{:S(2)}, u32[]{:S(2)}) collective-permute-start(bf16[2,8,2,16,512]{4,3,2,1,0:T(8,128)(2,1)} %collective-permute-done.7.refs_10_), channel_id=1, source_target_pairs={{0,2},{2,0},{12,14},{14,12},{1,3},{3,1},{13,15},{15,13},{16,18},{1... | collective-permute-start | bytes 1572872 | tf_op jit(solution)/shard_map/ppermute | solution.py:277
  102.6 22.7 %copy-start.1 = (bf16[2,8,256,128]{3,2,1,0:T(8,128)(2,1)S(1)}, bf16[2,8,256,128]{3,2,1,0:T(8,128)(2,1)}, u32[]{:S(2)}) copy-start(bf16[2,8,256,128]{3,2,1,0:T(8,128)(2,1)} %banded.1.refs_14_) | copy-start | bytes 3145732
  102.6 22.6 %collective-permute-start.2 = (bf16[1,8,2,16,512]{4,3,2,1,0:T(8,128)(2,1)S(1)}, bf16[1,8,2,16,512]{4,3,2,1,0:T(8,128)(2,1)S(1)}, u32[]{:S(2)}, u32[]{:S(2)}) collective-permute-start(bf16[1,8,2,16,512]{4,3,2,1,0:T(8,128)(2,1)S(1)} %slice.16), channel_id=1, source_target_pairs={{0,2},{2,0},{4,6},{6,4},{8,10},{10,8},{12,14},{14,12},{1,3},{3,1},... | collective-permute-start | bytes 786440 | tf_op jit(solution)/shard_map/ppermute | solution.py:277
  104.2 21.0 %collective-permute-start.3 = (bf16[1,8,2,16,512]{4,3,2,1,0:T(8,128)(2,1)S(1)}, bf16[1,8,2,16,512]{4,3,2,1,0:T(8,128)(2,1)S(1)}, u32[]{:S(2)}, u32[]{:S(2)}) collective-permute-start(bf16[1,8,2,16,512]{4,3,2,1,0:T(8,128)(2,1)S(1)} %slice.17), channel_id=1, source_target_pairs={{0,4},{2,6},{4,0},{6,2},{8,12},{10,14},{12,8},{14,10},{1,5},{3,7},... | collective-permute-start | bytes 786440 | tf_op jit(solution)/shard_map/ppermute | solution.py:277
  104.3 1.2 copy-start
  105.5 0.9 copy-start.5
  106.4 1.2 copy-start.6
  107.7 17.6 %copy-start.2 = (bf16[2,8,2,16,512]{4,3,2,1,0:T(8,128)(2,1)S(1)}, bf16[2,8,2,16,512]{4,3,2,1,0:T(8,128)(2,1)}, u32[]{:S(2)}) copy-start(bf16[2,8,2,16,512]{4,3,2,1,0:T(8,128)(2,1)} %first_stage.2.refs_2_) | copy-start | bytes 1572868
  107.7 17.7 %copy-start.7 = (bf16[8,256,256]{2,1,0:T(8,128)(2,1)S(1)}, bf16[8,256,256]{2,1,0:T(8,128)(2,1)}, u32[]{:S(2)}) copy-start(bf16[8,256,256]{2,1,0:T(8,128)(2,1)} %constant.64.clone.refs_13_) | copy-start | bytes 3145732
  134.2 2.7 %collective-permute-start.20 = (bf16[4096,128]{1,0:T(8,128)(2,1)S(1)}, bf16[4096,128]{1,0:T(8,128)(2,1)S(1)}, u32[]{:S(2)}, u32[]{:S(2)}) collective-permute-start(bf16[4096,128]{1,0:T(8,128)(2,1)S(1)} %get-tuple-element.14), channel_id=1, source_target_pairs={{0,1},{1,0},{2,3},{3,2},{4,5},{5,4},{6,7},{7,6},{8,9},{9,8},{10,11... | collective-permute-start | bytes 3145736 | tf_op jit(solution)/shard_map/ppermute | solution.py:615

commit v2 on v1

--- a/solution.py
+++ b/solution.py
@@ -265,13 +265,12 @@
     )(samples, tables)
 
 
-def gathered(own):
+def gathered(own, number):
     near = [(i, i ^ PAIR) for i in range(PAIR * LINE)]
     far = [(i, i ^ (2 * PAIR)) for i in range(PAIR * LINE)]
     flip = [(i, i ^ 1) for i in range(PAIR * LINE)]
     middle = [(i, i ^ (3 * PAIR)) for i in range(PAIR, 3 * PAIR)]
     ends = [(i, i ^ PAIR) for i in range(PAIR, 3 * PAIR)]
-    half = own.shape[0] // 2
 
     def send(array, route):
         return lax.ppermute(array, "freq", route)
@@ -280,10 +279,10 @@
     crossed = send(own, middle)
     by_flip = send(own, flip)
     by_far = send(own, far)
-    low = by_near[:half]
-    high = by_flip[half:]
-    near_low = send(low, flip)
-    near_high = send(high, near)
+    if number % 2:
+        near_flip = send(by_flip, near)
+    else:
+        near_flip = send(by_near, flip)
     far_flip = send(by_far, flip)
     relayed = send(by_far, ends)
     flip_middle = send(crossed, [pair for pair in flip if pair[0] in dict(middle)])
@@ -292,8 +291,7 @@
         (0, 0, own),
         (1, 0, by_flip),
         (PAIR, 0, by_near),
-        (PAIR + 1, 0, near_low),
-        (PAIR + 1, half, near_high),
+        (PAIR + 1, 0, near_flip),
         (2 * PAIR, 0, by_far),
         (2 * PAIR + 1, 0, far_flip),
         (3 * PAIR, 0, crossed, relayed),
@@ -583,8 +581,8 @@
     bands = banded(kernels)
 
     slots = []
-    for own in turned:
-        slots.append(gathered(own))
+    for number, own in enumerate(turned):
+        slots.append(gathered(own, number))
 
     bins = jnp.remainder(
         lax.axis_index("freq") * blocks_here + offsets.reshape(segs * kinds), ranks * blocks_here

time: 139 us -> 129 us (0.928)
  waiting for transfers between devices: 65.2 us -> 53.2 us
  starting transfers between devices: 39 us -> 43.4 us
  local copies, waits for them, and re-layouts: 5.06 us -> 2.64 us
    ppermute x20 -> x18, waiting for transfers between devices: 62.5 us -> 50.5 us  [send(): return lax.ppermute(array, 'freq', route)]
    ppermute x20 -> x18, starting transfers between devices: 38.9 us -> 43.4 us  [send(): return lax.ppermute(array, 'freq', route)]
    unnamed x22 -> x18, local copies, waits for them, and re-layouts: 4.12 us -> 2.48 us
  transfers between devices with their start and end apart: 21 -> 19, of which waited for: 5 -> 6; matrix products, arithmetic and copies ran while one was open for 1% -> 0% of each run, Pallas kernels for 10% -> 11%
where the time goes in v2:
time: 129 us
  waiting for transfers between devices  53.2 us (41%)
  starting transfers between devices  43.4 us (34%)
  Pallas kernels  27.6 us (21%)
  local copies, waits for them, and re-layouts  2.64 us (2%)
  other arithmetic  1.71 us (1%)
    ppermute x18, waiting for transfers between devices, send(): return lax.ppermute(array, 'freq', route)  50.5 us
    ppermute x18, starting transfers between devices, send(): return lax.ppermute(array, 'freq', route)  43.4 us
    pallas_call x2, Pallas kernels, chunk(): pl.pallas_call(functools.partial(chunk_kernel, plan), out_shape=out_shape...  16.5 us
    pallas_call x2, Pallas kernels, first_stage(): pl.pallas_call(functools.partial(first_kernel, begin, heights), out_shape...  8.81 us
    ppermute x1, waiting for transfers between devices, line_body(): other = lax.ppermute(send, 'seg', [(i, 1 - i) for i in range(2)])  2.65 us
  transfers between devices with their start and end apart: 19, of which 6 were waited for; matrix products, arithmetic and copies ran while one was open for 0% of the time, Pallas kernels for 11%

profile of v2, /device:TPU:0, one launch (start us, length us, event | category | flops | bytes accessed | tf_op | source)
XLA Modules:
  0.0 128.8 jit_solution(5150722043797911007)
XLA Ops:
  0.0 4.4 %first_stage.3.refs_2_ = bf16[2,8,2,16,512]{4,3,2,1,0:T(8,128)(2,1)} custom-call(f32[2,2,128,1024]{3,2,1,0:T(8,128)} %x_hbm.3, f32[288,1024]{1,0:T(8,128)} %constant.63.clone.tables_hbm), custom_call_target="tpu_custom_call" | custom-call | flops 1073741824 | bytes 2097152 | tf_op jit(solution)/shard_map/first_stage/pallas_call | solution.py:246
  4.4 0.0 copy-start.6
  4.4 0.0 copy-start.7
  4.4 0.0 copy-start.8
  4.5 4.1 %collective-permute-start.12 = (bf16[2,8,2,16,512]{4,3,2,1,0:T(8,128)(2,1)}, bf16[2,8,2,16,512]{4,3,2,1,0:T(8,128)(2,1)S(1)}, u32[]{:S(2)}, u32[]{:S(2)}) collective-permute-start(bf16[2,8,2,16,512]{4,3,2,1,0:T(8,128)(2,1)} %first_stage.3.refs_2_), channel_id=1, source_target_pairs={{0,8},{2,10},{4,12},{6,14},{8,0},{10,2},{12,4},{14,6},{1,9},{3,11}... | collective-permute-start | bytes 1572872 | tf_op jit(solution)/shard_map/ppermute | solution.py:276
  8.6 1.6 %collective-permute-start.10 = (bf16[2,8,2,16,512]{4,3,2,1,0:T(8,128)(2,1)}, bf16[2,8,2,16,512]{4,3,2,1,0:T(8,128)(2,1)S(1)}, u32[]{:S(2)}, u32[]{:S(2)}) collective-permute-start(bf16[2,8,2,16,512]{4,3,2,1,0:T(8,128)(2,1)} %first_stage.3.refs_2_), channel_id=1, source_target_pairs={{0,4},{2,6},{4,0},{6,2},{8,12},{10,14},{12,8},{14,10},{1,5},{3,7},... | collective-permute-start | bytes 1572872 | tf_op jit(solution)/shard_map/ppermute | solution.py:276
  10.2 1.5 %collective-permute-start.14 = (bf16[2,8,2,16,512]{4,3,2,1,0:T(8,128)(2,1)}, bf16[2,8,2,16,512]{4,3,2,1,0:T(8,128)(2,1)}, u32[]{:S(2)}, u32[]{:S(2)}) collective-permute-start(bf16[2,8,2,16,512]{4,3,2,1,0:T(8,128)(2,1)} %first_stage.3.refs_2_), channel_id=1, source_target_pairs={{4,8},{6,10},{8,4},{10,6},{5,9},{7,11},{9,5},{11,7},{20,24},{22,26... | collective-permute-start | bytes 1572872 | tf_op jit(solution)/shard_map/ppermute | solution.py:276
  11.6 1.5 %collective-permute-start.9 = (bf16[2,8,2,16,512]{4,3,2,1,0:T(8,128)(2,1)}, bf16[2,8,2,16,512]{4,3,2,1,0:T(8,128)(2,1)}, u32[]{:S(2)}, u32[]{:S(2)}) collective-permute-start(bf16[2,8,2,16,512]{4,3,2,1,0:T(8,128)(2,1)} %first_stage.3.refs_2_), channel_id=1, source_target_pairs={{0,2},{2,0},{4,6},{6,4},{8,10},{10,8},{12,14},{14,12},{1,3},{3,1},... | collective-permute-start | bytes 1572872 | tf_op jit(solution)/shard_map/ppermute | solution.py:276
  13.1 4.4 %first_stage.2.refs_2_ = bf16[2,8,2,16,512]{4,3,2,1,0:T(8,128)(2,1)} custom-call(f32[2,2,128,1024]{3,2,1,0:T(8,128)} %x_hbm.3, f32[288,1024]{1,0:T(8,128)} %constant.63.clone.tables_hbm), custom_call_target="tpu_custom_call" | custom-call | flops 1073741824 | bytes 2097152 | tf_op jit(solution)/shard_map/first_stage/pallas_call | solution.py:246
  17.5 2.5 %collective-permute-start.3 = (bf16[2,8,2,16,512]{4,3,2,1,0:T(8,128)(2,1)}, bf16[2,8,2,16,512]{4,3,2,1,0:T(8,128)(2,1)S(1)}, u32[]{:S(2)}, u32[]{:S(2)}) collective-permute-start(bf16[2,8,2,16,512]{4,3,2,1,0:T(8,128)(2,1)} %first_stage.2.refs_2_), channel_id=1, source_target_pairs={{0,8},{2,10},{4,12},{6,14},{8,0},{10,2},{12,4},{14,6},{1,9},{3,11}... | collective-permute-start | bytes 1572872 | tf_op jit(solution)/shard_map/ppermute | solution.py:276
  20.0 13.7 %collective-permute-done.12.refs_6_ = bf16[2,8,2,16,512]{4,3,2,1,0:T(8,128)(2,1)S(1)} collective-permute-done((bf16[2,8,2,16,512]{4,3,2,1,0:T(8,128)(2,1)}, bf16[2,8,2,16,512]{4,3,2,1,0:T(8,128)(2,1)S(1)}, u32[]{:S(2)}, u32[]{:S(2)}) %collective-permute-start.12) | collective-permute-done | bytes 524320 | tf_op jit(solution)/shard_map/ppermute | solution.py:276
  33.7 2.0 %collective-permute-start = (bf16[2,8,2,16,512]{4,3,2,1,0:T(8,128)(2,1)}, bf16[2,8,2,16,512]{4,3,2,1,0:T(8,128)(2,1)S(1)}, u32[]{:S(2)}, u32[]{:S(2)}) collective-permute-start(bf16[2,8,2,16,512]{4,3,2,1,0:T(8,128)(2,1)} %first_stage.2.refs_2_), channel_id=1, source_target_pairs={{0,2},{2,0},{4,6},{6,4},{8,10},{10,8},{12,14},{14,12},{1,3},{3,1},... | collective-permute-start | bytes 1572872 | tf_op jit(solution)/shard_map/ppermute | solution.py:276
  35.8 0.0 collective-permute-done.10.refs_4_
  35.8 0.7 collective-permute-start.5
  36.5 1.3 %collective-permute-start.15 = (bf16[2,8,2,16,512]{4,3,2,1,0:T(8,128)(2,1)S(1)}, bf16[2,8,2,16,512]{4,3,2,1,0:T(8,128)(2,1)}, u32[]{:S(2)}, u32[]{:S(2)}) collective-permute-start(bf16[2,8,2,16,512]{4,3,2,1,0:T(8,128)(2,1)S(1)} %collective-permute-done.12.refs_6_), channel_id=1, source_target_pairs={{4,0},{6,2},{8,12},{10,14},{5,1},{7,3},{9,13},{11,15},{20,16},{22,... | collective-permute-start | bytes 1572872 | tf_op jit(solution)/shard_map/ppermute | solution.py:276
  37.8 0.0 collective-permute-done.9.refs_3_
  37.8 0.1 collective-permute-start.13
  37.9 28.8 %collective-permute-done.3.refs_6_ = bf16[2,8,2,16,512]{4,3,2,1,0:T(8,128)(2,1)S(1)} collective-permute-done((bf16[2,8,2,16,512]{4,3,2,1,0:T(8,128)(2,1)}, bf16[2,8,2,16,512]{4,3,2,1,0:T(8,128)(2,1)S(1)}, u32[]{:S(2)}, u32[]{:S(2)}) %collective-permute-start.3) | collective-permute-done | bytes 524320 | tf_op jit(solution)/shard_map/ppermute | solution.py:276
  66.6 1.8 %collective-permute-start.11 = (bf16[2,8,2,16,512]{4,3,2,1,0:T(8,128)(2,1)S(1)}, bf16[2,8,2,16,512]{4,3,2,1,0:T(8,128)(2,1)}, u32[]{:S(2)}, u32[]{:S(2)}) collective-permute-start(bf16[2,8,2,16,512]{4,3,2,1,0:T(8,128)(2,1)S(1)} %collective-permute-done.10.refs_4_), channel_id=1, source_target_pairs={{0,2},{2,0},{4,6},{6,4},{8,10},{10,8},{12,14},{14,12},{1,3},{3,1},... | collective-permute-start | bytes 1572872 | tf_op jit(solution)/shard_map/ppermute | solution.py:276
  68.4 0.0 collective-permute-done.refs_3_
  68.4 1.5 %collective-permute-start.16 = (bf16[2,8,2,16,512]{4,3,2,1,0:T(8,128)(2,1)}, bf16[2,8,2,16,512]{4,3,2,1,0:T(8,128)(2,1)}, u32[]{:S(2)}, u32[]{:S(2)}) collective-permute-start(bf16[2,8,2,16,512]{4,3,2,1,0:T(8,128)(2,1)} %collective-permute-done.14.refs_8_), channel_id=1, source_target_pairs={{4,6},{6,4},{8,10},{10,8},{5,7},{7,5},{9,11},{11,9},{20,22},{22,20... | collective-permute-start | bytes 1572872 | tf_op jit(solution)/shard_map/ppermute | solution.py:276
  69.9 0.0 collective-permute-done.5.refs_8_
  69.9 1.3 collective-permute-start.6
  71.2 5.9 %collective-permute-done.15.refs_9_ = bf16[2,8,2,16,512]{4,3,2,1,0:T(8,128)(2,1)} collective-permute-done((bf16[2,8,2,16,512]{4,3,2,1,0:T(8,128)(2,1)S(1)}, bf16[2,8,2,16,512]{4,3,2,1,0:T(8,128)(2,1)}, u32[]{:S(2)}, u32[]{:S(2)}) %collective-permute-start.15) | collective-permute-done | bytes 524320 | tf_op jit(solution)/shard_map/ppermute | solution.py:276
  77.1 3.4 %collective-permute-start.17 = (bf16[2,8,2,16,512]{4,3,2,1,0:T(8,128)(2,1)}, bf16[2,8,2,16,512]{4,3,2,1,0:T(8,128)(2,1)}, u32[]{:S(2)}, u32[]{:S(2)}) collective-permute-start(bf16[2,8,2,16,512]{4,3,2,1,0:T(8,128)(2,1)} %collective-permute-done.15.refs_9_), channel_id=1, source_target_pairs={{0,2},{2,0},{12,14},{14,12},{1,3},{3,1},{13,15},{15,13},{16,18},{1... | collective-permute-start | bytes 1572872 | tf_op jit(solution)/shard_map/ppermute | solution.py:276
  80.5 0.1 add.22
  80.6 0.0 collective-permute-done.13.refs_7_
  80.6 0.9 collective-permute-start.1
  81.5 0.0 collective-permute-done.11.refs_5_
  81.5 1.5 %collective-permute-start.4 = (bf16[2,8,2,16,512]{4,3,2,1,0:T(8,128)(2,1)S(1)}, bf16[2,8,2,16,512]{4,3,2,1,0:T(8,128)(2,1)}, u32[]{:S(2)}, u32[]{:S(2)}) collective-permute-start(bf16[2,8,2,16,512]{4,3,2,1,0:T(8,128)(2,1)S(1)} %collective-permute-done.3.refs_6_), channel_id=1, source_target_pairs={{0,2},{2,0},{4,6},{6,4},{8,10},{10,8},{12,14},{14,12},{1,3},{3,1},... | collective-permute-start | bytes 1572872 | tf_op jit(solution)/shard_map/ppermute | solution.py:276
  83.0 0.0 collective-permute-done.16.refs_10_
  83.0 12.4 %collective-permute-start.2 = (bf16[2,8,2,16,512]{4,3,2,1,0:T(8,128)(2,1)S(1)}, bf16[2,8,2,16,512]{4,3,2,1,0:T(8,128)(2,1)}, u32[]{:S(2)}, u32[]{:S(2)}) collective-permute-start(bf16[2,8,2,16,512]{4,3,2,1,0:T(8,128)(2,1)S(1)} %collective-permute-done.refs_3_), channel_id=1, source_target_pairs={{0,4},{2,6},{4,0},{6,2},{8,12},{10,14},{12,8},{14,10},{1,5},{3,7},... | collective-permute-start | bytes 1572872 | tf_op jit(solution)/shard_map/ppermute | solution.py:276
  95.5 1.5 %collective-permute-start.7 = (bf16[2,8,2,16,512]{4,3,2,1,0:T(8,128)(2,1)S(1)}, bf16[2,8,2,16,512]{4,3,2,1,0:T(8,128)(2,1)}, u32[]{:S(2)}, u32[]{:S(2)}) collective-permute-start(bf16[2,8,2,16,512]{4,3,2,1,0:T(8,128)(2,1)S(1)} %collective-permute-done.5.refs_8_), channel_id=1, source_target_pairs={{4,6},{6,4},{8,10},{10,8},{5,7},{7,5},{9,11},{11,9},{20,22},{22,20... | collective-permute-start | bytes 1572872 | tf_op jit(solution)/shard_map/ppermute | solution.py:276
  96.9 3.9 %collective-permute-start.8 = (bf16[2,8,2,16,512]{4,3,2,1,0:T(8,128)(2,1)}, bf16[2,8,2,16,512]{4,3,2,1,0:T(8,128)(2,1)}, u32[]{:S(2)}, u32[]{:S(2)}) collective-permute-start(bf16[2,8,2,16,512]{4,3,2,1,0:T(8,128)(2,1)} %collective-permute-done.6.refs_9_), channel_id=1, source_target_pairs={{0,2},{2,0},{12,14},{14,12},{1,3},{3,1},{13,15},{15,13},{16,18},{1... | collective-permute-start | bytes 1572872 | tf_op jit(solution)/shard_map/ppermute | solution.py:276
  100.8 0.2 fusion
  101.0 2.2 %banded.1.refs_13_ = bf16[2,8,256,128]{3,2,1,0:T(8,128)(2,1)} custom-call(bf16[2,8,128]{2,1,0:T(8,128)(2,1)} %kernels.1), custom_call_target="tpu_custom_call" | custom-call | tf_op jit(solution)/shard_map/banded/pallas_call | solution.py:490
  103.3 0.1 concatenate.3.refs_0_
  103.4 0.0 copy-start
  103.4 1.2 copy-done
  104.6 1.2 copy-done.4
  105.8 7.5 %chunk.2 = (f32[8,8,128,128]{3,2,1,0:T(8,128)S(1)}, bf16[2,2,1152,128]{3,2,1,0:T(8,128)(2,1)S(1)}, bf16[2,2,1152,128]{3,2,1,0:T(8,128)(2,1)S(1)}) custom-call(s32[50]{0:T(128)S(1)} %concatenate.3.refs_0_, f32[2]{0:T(128)S(1)} %broadcast_multiply_fusion.refs_1_, bf16[2,8,2,16,512]{4,3,2,1,0:T(8,128)(2,1)S(1)} %copy-done.3, ...), custom_call_target="tpu_custom_call" | custom-call | flops 2885681152 | bytes 8388608 | tf_op jit(solution)/shard_map/chunk/pallas_call | solution.py:540
  113.4 0.0 collective-permute-done.1.refs_4_
  113.4 0.3 collective-permute-done.2.refs_5_
  113.7 1.8 %collective-permute-done.8.refs_11_ = bf16[2,8,2,16,512]{4,3,2,1,0:T(8,128)(2,1)} collective-permute-done((bf16[2,8,2,16,512]{4,3,2,1,0:T(8,128)(2,1)}, bf16[2,8,2,16,512]{4,3,2,1,0:T(8,128)(2,1)}, u32[]{:S(2)}, u32[]{:S(2)}) %collective-permute-start.8) | collective-permute-done | bytes 524320 | tf_op jit(solution)/shard_map/ppermute | solution.py:276
  115.6 9.0 %chunk.3 = (f32[4096,128]{1,0:T(8,128)S(1)}, bf16[4096,128]{1,0:T(8,128)(2,1)S(1)}) custom-call(s32[50]{0:T(128)S(1)} %concatenate.3.refs_0_, f32[2]{0:T(128)S(1)} %broadcast_multiply_fusion.refs_1_, bf16[2,8,2,16,512]{4,3,2,1,0:T(8,128)(2,1)S(1)} %copy-done.2, bf16[2,8,2,16,512]{4,3,2,1,0:T(8,128)(2,1)S(1)} %collective-permute-done.refs_3_, ...), custom_call_target="tpu_custom_call" | custom-call | flops 4093640704 | bytes 8388608 | tf_op jit(solution)/shard_map/chunk/pallas_call | solution.py:540
  124.6 0.1 collective-permute-start.18
  124.7 2.6 %collective-permute-done.18 = bf16[4096,128]{1,0:T(8,128)(2,1)S(1)} collective-permute-done((bf16[4096,128]{1,0:T(8,128)(2,1)S(1)}, bf16[4096,128]{1,0:T(8,128)(2,1)S(1)}, u32[]{:S(2)}, u32[]{:S(2)}) %collective-permute-start.18) | collective-permute-done | bytes 1048608 | tf_op jit(solution)/shard_map/ppermute | solution.py:613
  127.3 1.5 %convert_add_fusion = f32[4096,128]{1,0:T(8,128)} fusion(f32[4096,128]{1,0:T(8,128)S(1)} %get-tuple-element.13, bf16[4096,128]{1,0:T(8,128)(2,1)S(1)} %collective-permute-done.18), kind=kLoop, calls=%fused_computation | loop fusion | flops 1048576 | bytes 5242880 | tf_op jit(solution)/shard_map/add | solution.py:614
  (21 shorter events, 0.1 us)
Async XLA Ops:
  4.4 76.1 %copy-start.6 = (s32[2,8]{1,0:T(2,128)S(1)}, s32[2,8]{1,0:T(2,128)}, u32[]{:S(2)}) copy-start(s32[2,8]{1,0:T(2,128)} %param.9) | copy-start | bytes 196
  4.4 96.4 %copy-start.7 = (f32[16]{0:T(128)S(1)}, f32[16]{0:T(128)}, u32[]{:S(2)}) copy-start(f32[16]{0:T(128)} %param.11) | copy-start | bytes 196
  4.4 96.4 %copy-start.8 = (s32[2]{0:T(128)S(1)}, s32[2]{0:T(128)}, u32[]{:S(2)}) copy-start(s32[2]{0:T(128)} %param.10) | copy-start | bytes 28
  4.5 98.9 %copy-start.3 = (bf16[2,8,2,16,512]{4,3,2,1,0:T(8,128)(2,1)S(1)}, bf16[2,8,2,16,512]{4,3,2,1,0:T(8,128)(2,1)}, u32[]{:S(2)}) copy-start(bf16[2,8,2,16,512]{4,3,2,1,0:T(8,128)(2,1)} %first_stage.3.refs_2_) | copy-start | bytes 1572868
  4.5 29.2 %collective-permute-start.12 = (bf16[2,8,2,16,512]{4,3,2,1,0:T(8,128)(2,1)}, bf16[2,8,2,16,512]{4,3,2,1,0:T(8,128)(2,1)S(1)}, u32[]{:S(2)}, u32[]{:S(2)}) collective-permute-start(bf16[2,8,2,16,512]{4,3,2,1,0:T(8,128)(2,1)} %first_stage.3.refs_2_), channel_id=1, source_target_pairs={{0,8},{2,10},{4,12},{6,14},{8,0},{10,2},{12,4},{14,6},{1,9},{3,11}... | collective-permute-start | bytes 1572872 | tf_op jit(solution)/shard_map/ppermute | solution.py:276
  8.6 27.2 %collective-permute-start.10 = (bf16[2,8,2,16,512]{4,3,2,1,0:T(8,128)(2,1)}, bf16[2,8,2,16,512]{4,3,2,1,0:T(8,128)(2,1)S(1)}, u32[]{:S(2)}, u32[]{:S(2)}) collective-permute-start(bf16[2,8,2,16,512]{4,3,2,1,0:T(8,128)(2,1)} %first_stage.3.refs_2_), channel_id=1, source_target_pairs={{0,4},{2,6},{4,0},{6,2},{8,12},{10,14},{12,8},{14,10},{1,5},{3,7},... | collective-permute-start | bytes 1572872 | tf_op jit(solution)/shard_map/ppermute | solution.py:276
  10.2 26.3 %collective-permute-start.14 = (bf16[2,8,2,16,512]{4,3,2,1,0:T(8,128)(2,1)}, bf16[2,8,2,16,512]{4,3,2,1,0:T(8,128)(2,1)}, u32[]{:S(2)}, u32[]{:S(2)}) collective-permute-start(bf16[2,8,2,16,512]{4,3,2,1,0:T(8,128)(2,1)} %first_stage.3.refs_2_), channel_id=1, source_target_pairs={{4,8},{6,10},{8,4},{10,6},{5,9},{7,11},{9,5},{11,7},{20,24},{22,26... | collective-permute-start | bytes 1572872 | tf_op jit(solution)/shard_map/ppermute | solution.py:276
  11.6 26.1 %collective-permute-start.9 = (bf16[2,8,2,16,512]{4,3,2,1,0:T(8,128)(2,1)}, bf16[2,8,2,16,512]{4,3,2,1,0:T(8,128)(2,1)}, u32[]{:S(2)}, u32[]{:S(2)}) collective-permute-start(bf16[2,8,2,16,512]{4,3,2,1,0:T(8,128)(2,1)} %first_stage.3.refs_2_), channel_id=1, source_target_pairs={{0,2},{2,0},{4,6},{6,4},{8,10},{10,8},{12,14},{14,12},{1,3},{3,1},... | collective-permute-start | bytes 1572872 | tf_op jit(solution)/shard_map/ppermute | solution.py:276
  17.5 49.1 %collective-permute-start.3 = (bf16[2,8,2,16,512]{4,3,2,1,0:T(8,128)(2,1)}, bf16[2,8,2,16,512]{4,3,2,1,0:T(8,128)(2,1)S(1)}, u32[]{:S(2)}, u32[]{:S(2)}) collective-permute-start(bf16[2,8,2,16,512]{4,3,2,1,0:T(8,128)(2,1)} %first_stage.2.refs_2_), channel_id=1, source_target_pairs={{0,8},{2,10},{4,12},{6,14},{8,0},{10,2},{12,4},{14,6},{1,9},{3,11}... | collective-permute-start | bytes 1572872 | tf_op jit(solution)/shard_map/ppermute | solution.py:276
  33.7 34.7 %collective-permute-start = (bf16[2,8,2,16,512]{4,3,2,1,0:T(8,128)(2,1)}, bf16[2,8,2,16,512]{4,3,2,1,0:T(8,128)(2,1)S(1)}, u32[]{:S(2)}, u32[]{:S(2)}) collective-permute-start(bf16[2,8,2,16,512]{4,3,2,1,0:T(8,128)(2,1)} %first_stage.2.refs_2_), channel_id=1, source_target_pairs={{0,2},{2,0},{4,6},{6,4},{8,10},{10,8},{12,14},{14,12},{1,3},{3,1},... | collective-permute-start | bytes 1572872 | tf_op jit(solution)/shard_map/ppermute | solution.py:276
  35.8 34.1 %collective-permute-start.5 = (bf16[2,8,2,16,512]{4,3,2,1,0:T(8,128)(2,1)}, bf16[2,8,2,16,512]{4,3,2,1,0:T(8,128)(2,1)S(1)}, u32[]{:S(2)}, u32[]{:S(2)}) collective-permute-start(bf16[2,8,2,16,512]{4,3,2,1,0:T(8,128)(2,1)} %first_stage.2.refs_2_), channel_id=1, source_target_pairs={{4,8},{6,10},{8,4},{10,6},{5,9},{7,11},{9,5},{11,7},{20,24},{22,26... | collective-permute-start | bytes 1572872 | tf_op jit(solution)/shard_map/ppermute | solution.py:276
  36.5 40.6 %collective-permute-start.15 = (bf16[2,8,2,16,512]{4,3,2,1,0:T(8,128)(2,1)S(1)}, bf16[2,8,2,16,512]{4,3,2,1,0:T(8,128)(2,1)}, u32[]{:S(2)}, u32[]{:S(2)}) collective-permute-start(bf16[2,8,2,16,512]{4,3,2,1,0:T(8,128)(2,1)S(1)} %collective-permute-done.12.refs_6_), channel_id=1, source_target_pairs={{4,0},{6,2},{8,12},{10,14},{5,1},{7,3},{9,13},{11,15},{20,16},{22,... | collective-permute-start | bytes 1572872 | tf_op jit(solution)/shard_map/ppermute | solution.py:276
  37.8 42.9 %collective-permute-start.13 = (bf16[2,8,2,16,512]{4,3,2,1,0:T(8,128)(2,1)S(1)}, bf16[2,8,2,16,512]{4,3,2,1,0:T(8,128)(2,1)}, u32[]{:S(2)}, u32[]{:S(2)}) collective-permute-start(bf16[2,8,2,16,512]{4,3,2,1,0:T(8,128)(2,1)S(1)} %collective-permute-done.12.refs_6_), channel_id=1, source_target_pairs={{0,2},{2,0},{4,6},{6,4},{8,10},{10,8},{12,14},{14,12},{1,3},{3,1},... | collective-permute-start | bytes 1572872 | tf_op jit(solution)/shard_map/ppermute | solution.py:276
  66.6 14.9 %collective-permute-start.11 = (bf16[2,8,2,16,512]{4,3,2,1,0:T(8,128)(2,1)S(1)}, bf16[2,8,2,16,512]{4,3,2,1,0:T(8,128)(2,1)}, u32[]{:S(2)}, u32[]{:S(2)}) collective-permute-start(bf16[2,8,2,16,512]{4,3,2,1,0:T(8,128)(2,1)S(1)} %collective-permute-done.10.refs_4_), channel_id=1, source_target_pairs={{0,2},{2,0},{4,6},{6,4},{8,10},{10,8},{12,14},{14,12},{1,3},{3,1},... | collective-permute-start | bytes 1572872 | tf_op jit(solution)/shard_map/ppermute | solution.py:276
  68.4 14.6 %collective-permute-start.16 = (bf16[2,8,2,16,512]{4,3,2,1,0:T(8,128)(2,1)}, bf16[2,8,2,16,512]{4,3,2,1,0:T(8,128)(2,1)}, u32[]{:S(2)}, u32[]{:S(2)}) collective-permute-start(bf16[2,8,2,16,512]{4,3,2,1,0:T(8,128)(2,1)} %collective-permute-done.14.refs_8_), channel_id=1, source_target_pairs={{4,6},{6,4},{8,10},{10,8},{5,7},{7,5},{9,11},{11,9},{20,22},{22,20... | collective-permute-start | bytes 1572872 | tf_op jit(solution)/shard_map/ppermute | solution.py:276
  69.9 25.6 %collective-permute-start.6 = (bf16[2,8,2,16,512]{4,3,2,1,0:T(8,128)(2,1)S(1)}, bf16[2,8,2,16,512]{4,3,2,1,0:T(8,128)(2,1)}, u32[]{:S(2)}, u32[]{:S(2)}) collective-permute-start(bf16[2,8,2,16,512]{4,3,2,1,0:T(8,128)(2,1)S(1)} %collective-permute-done.3.refs_6_), channel_id=1, source_target_pairs={{4,0},{6,2},{8,12},{10,14},{5,1},{7,3},{9,13},{11,15},{20,16},{22,... | collective-permute-start | bytes 1572872 | tf_op jit(solution)/shard_map/ppermute | solution.py:276
  77.1 19.9 %collective-permute-start.17 = (bf16[2,8,2,16,512]{4,3,2,1,0:T(8,128)(2,1)}, bf16[2,8,2,16,512]{4,3,2,1,0:T(8,128)(2,1)}, u32[]{:S(2)}, u32[]{:S(2)}) collective-permute-start(bf16[2,8,2,16,512]{4,3,2,1,0:T(8,128)(2,1)} %collective-permute-done.15.refs_9_), channel_id=1, source_target_pairs={{0,2},{2,0},{12,14},{14,12},{1,3},{3,1},{13,15},{15,13},{16,18},{1... | collective-permute-start | bytes 1572872 | tf_op jit(solution)/shard_map/ppermute | solution.py:276
  80.6 32.7 %collective-permute-start.1 = (bf16[2,8,2,16,512]{4,3,2,1,0:T(8,128)(2,1)}, bf16[2,8,2,16,512]{4,3,2,1,0:T(8,128)(2,1)}, u32[]{:S(2)}, u32[]{:S(2)}) collective-permute-start(bf16[2,8,2,16,512]{4,3,2,1,0:T(8,128)(2,1)} %first_stage.2.refs_2_), channel_id=1, source_target_pairs={{0,4},{2,6},{4,0},{6,2},{8,12},{10,14},{12,8},{14,10},{1,5},{3,7},... | collective-permute-start | bytes 1572872 | tf_op jit(solution)/shard_map/ppermute | solution.py:276
  81.5 31.8 %collective-permute-start.4 = (bf16[2,8,2,16,512]{4,3,2,1,0:T(8,128)(2,1)S(1)}, bf16[2,8,2,16,512]{4,3,2,1,0:T(8,128)(2,1)}, u32[]{:S(2)}, u32[]{:S(2)}) collective-permute-start(bf16[2,8,2,16,512]{4,3,2,1,0:T(8,128)(2,1)S(1)} %collective-permute-done.3.refs_6_), channel_id=1, source_target_pairs={{0,2},{2,0},{4,6},{6,4},{8,10},{10,8},{12,14},{14,12},{1,3},{3,1},... | collective-permute-start | bytes 1572872 | tf_op jit(solution)/shard_map/ppermute | solution.py:276
  83.0 30.7 %collective-permute-start.2 = (bf16[2,8,2,16,512]{4,3,2,1,0:T(8,128)(2,1)S(1)}, bf16[2,8,2,16,512]{4,3,2,1,0:T(8,128)(2,1)}, u32[]{:S(2)}, u32[]{:S(2)}) collective-permute-start(bf16[2,8,2,16,512]{4,3,2,1,0:T(8,128)(2,1)S(1)} %collective-permute-done.refs_3_), channel_id=1, source_target_pairs={{0,4},{2,6},{4,0},{6,2},{8,12},{10,14},{12,8},{14,10},{1,5},{3,7},... | collective-permute-start | bytes 1572872 | tf_op jit(solution)/shard_map/ppermute | solution.py:276
  95.5 18.3 %collective-permute-start.7 = (bf16[2,8,2,16,512]{4,3,2,1,0:T(8,128)(2,1)S(1)}, bf16[2,8,2,16,512]{4,3,2,1,0:T(8,128)(2,1)}, u32[]{:S(2)}, u32[]{:S(2)}) collective-permute-start(bf16[2,8,2,16,512]{4,3,2,1,0:T(8,128)(2,1)S(1)} %collective-permute-done.5.refs_8_), channel_id=1, source_target_pairs={{4,6},{6,4},{8,10},{10,8},{5,7},{7,5},{9,11},{11,9},{20,22},{22,20... | collective-permute-start | bytes 1572872 | tf_op jit(solution)/shard_map/ppermute | solution.py:276
  96.9 18.6 %collective-permute-start.8 = (bf16[2,8,2,16,512]{4,3,2,1,0:T(8,128)(2,1)}, bf16[2,8,2,16,512]{4,3,2,1,0:T(8,128)(2,1)}, u32[]{:S(2)}, u32[]{:S(2)}) collective-permute-start(bf16[2,8,2,16,512]{4,3,2,1,0:T(8,128)(2,1)} %collective-permute-done.6.refs_9_), channel_id=1, source_target_pairs={{0,2},{2,0},{12,14},{14,12},{1,3},{3,1},{13,15},{15,13},{16,18},{1... | collective-permute-start | bytes 1572872 | tf_op jit(solution)/shard_map/ppermute | solution.py:276
  103.4 1.2 copy-start
  104.6 1.2 copy-start.4
  105.8 9.8 %copy-start.1 = (bf16[2,8,256,128]{3,2,1,0:T(8,128)(2,1)S(1)}, bf16[2,8,256,128]{3,2,1,0:T(8,128)(2,1)}, u32[]{:S(2)}) copy-start(bf16[2,8,256,128]{3,2,1,0:T(8,128)(2,1)} %banded.1.refs_13_) | copy-start | bytes 3145732
  105.8 9.8 %copy-start.2 = (bf16[2,8,2,16,512]{4,3,2,1,0:T(8,128)(2,1)S(1)}, bf16[2,8,2,16,512]{4,3,2,1,0:T(8,128)(2,1)}, u32[]{:S(2)}) copy-start(bf16[2,8,2,16,512]{4,3,2,1,0:T(8,128)(2,1)} %first_stage.2.refs_2_) | copy-start | bytes 1572868
  105.8 9.8 %copy-start.5 = (bf16[8,256,256]{2,1,0:T(8,128)(2,1)S(1)}, bf16[8,256,256]{2,1,0:T(8,128)(2,1)}, u32[]{:S(2)}) copy-start(bf16[8,256,256]{2,1,0:T(8,128)(2,1)} %constant.64.clone.refs_12_) | copy-start | bytes 3145732
  124.6 2.7 %collective-permute-start.18 = (bf16[4096,128]{1,0:T(8,128)(2,1)S(1)}, bf16[4096,128]{1,0:T(8,128)(2,1)S(1)}, u32[]{:S(2)}, u32[]{:S(2)}) collective-permute-start(bf16[4096,128]{1,0:T(8,128)(2,1)S(1)} %get-tuple-element.14), channel_id=1, source_target_pairs={{0,1},{1,0},{2,3},{3,2},{4,5},{5,4},{6,7},{7,6},{8,9},{9,8},{10,11... | collective-permute-start | bytes 3145736 | tf_op jit(solution)/shard_map/ppermute | solution.py:613
